TPU v7x, 32 devices: a whole 2x2x4 slice. The times are simulated.
32 devices in a mesh: tab: 8 (over z, x), rep: 4 (over y, core).
Axes of the slice: x: 2, y: 2, z: 4, core: 2. Of those that a mesh axis runs over, the one named last changes fastest.
Arguments:
- sample_ids: int32 [16384, 26], P(('tab', 'rep')), may hold values from 0 to 4095, as said below
- features: bfloat16 [16384, 27, 128], P(('tab', 'rep')), may hold values from -6 to 6
- pair_grad: bfloat16 [351, 16384], P(None, ('tab', 'rep')), may hold values from -1.59375 to 1.59375
Outputs:
- table_grad: float32 [26, 4096, 128], P(None, ('tab', 'rep'))
- dense_grad: float32 [16384, 128], P(('tab', 'rep'))
Inputs may be any that keep to these rules, and one draw needn't show every extreme that they name: `sample_ids`: row r is owned by device r // 128, numbered tab * 4 + rep. For each field and the 512 samples of one device (aligned blocks of rows in device order), at most 32 ids fall in the rows of any one device, and at most 128 in the rows of any one tab index; in every block and field both bounds are reached.
All inputs are finite; a program needn't handle non-finite values.
Results may differ from a plain program's by a relative error of at most 0.0029.
Values may be sent and summed in bfloat16 or wider, within the bound.
No kernel may reach another device: no remote copies, remote signals or barrier semaphores. Data moves between devices by JAX's collectives and lax.ppermute only.
A program may use at most 128 MiB of HBM per device.

v0:
```python
import jax
import jax.numpy as jnp
import numpy as np
from jax import lax
from jax.sharding import PartitionSpec as P

RQ = 128


def pair_table(vectors):
    row_of, col_of = np.tril_indices(vectors, -1)
    spread = np.zeros((row_of.shape[0], vectors * vectors), np.float32)
    places = np.arange(row_of.shape[0])
    spread[places, row_of * vectors + col_of] = 1.0
    spread[places, col_of * vectors + row_of] = 1.0
    return spread


def arrival_order(targets, bins):
    matches = (targets[:, None] == jnp.arange(bins, dtype=jnp.int32)[None, :]).astype(jnp.int32)
    return jnp.sum(jnp.cumsum(matches, axis=0) * matches, axis=1) - 1


def place_field(slot_of, tag_of, grads, slot_total):
    placing = jnp.arange(slot_total, dtype=jnp.int32)[:, None] == slot_of[None, :]
    placed = jnp.dot(
        placing.astype(jnp.bfloat16), grads, preferred_element_type=jnp.float32
    ).astype(jnp.bfloat16)
    shifted = (tag_of + 1).astype(jnp.float32)
    tag_sum = jnp.dot(placing.astype(jnp.float32), shifted, precision=lax.Precision.HIGHEST)
    return (placed, tag_sum.astype(jnp.int32) - 1)


def tally_rows(arrived, row_tags, row_count):

    def per_field(pieces):
        slot_grads, slot_tags = pieces
        matches = (slot_tags[None, :] == jnp.arange(row_count, dtype=jnp.int32)[:, None]).astype(
            jnp.bfloat16
        )
        return jnp.dot(matches, slot_grads, preferred_element_type=jnp.float32)

    return lax.map(per_field, (arrived, row_tags))


def local(sample_ids, features, pair_grad):
    vectors = features.shape[1]
    samples = features.shape[0]
    depth = features.shape[2]
    spread = jnp.asarray(pair_table(vectors).T).astype(jnp.bfloat16)
    symmetric = jnp.dot(spread, pair_grad, preferred_element_type=jnp.float32)
    symmetric = symmetric.astype(jnp.bfloat16).reshape(vectors, vectors, samples)
    gradients = jnp.einsum("fgb,bge->fbe", symmetric, features, preferred_element_type=jnp.float32)
    dense_grad = gradients[0]
    field_grads = gradients[1:].astype(jnp.bfloat16)
    fields = vectors - 1
    col_count = lax.axis_size("tab")
    rep_count = lax.axis_size("rep")
    capacity = 2 * samples // (col_count * rep_count)
    slot_total = col_count * rep_count * capacity
    ids_by_field = sample_ids.T

    def build_owner(pieces):
        column_ids, grads = pieces
        owners = column_ids // RQ
        slot_of = owners * capacity + arrival_order(owners, col_count * rep_count)
        return place_field(slot_of, column_ids % RQ, grads, slot_total)

    outgoing, row_tags = lax.map(build_owner, (ids_by_field, field_grads))
    outgoing = outgoing.reshape(fields, col_count, rep_count, capacity, depth)
    row_tags = row_tags.reshape(fields, col_count, rep_count, capacity)
    arrived, tags_in = (
        lax.all_to_all(
            lax.all_to_all(outgoing, "tab", split_axis=1, concat_axis=1, tiled=True),
            "rep",
            split_axis=2,
            concat_axis=2,
            tiled=True,
        ),
        lax.all_to_all(
            lax.all_to_all(row_tags, "tab", split_axis=1, concat_axis=1, tiled=True),
            "rep",
            split_axis=2,
            concat_axis=2,
            tiled=True,
        ),
    )
    table_grad = tally_rows(arrived.reshape(fields, -1, depth), tags_in.reshape(fields, -1), RQ)
    return (table_grad, dense_grad)


def solution(mesh):
    placed = (P(("tab", "rep"), None), P(("tab", "rep"), None, None), P(None, ("tab", "rep")))
    return jax.shard_map(
        local,
        mesh=mesh,
        in_specs=placed,
        out_specs=(P(None, ("tab", "rep"), None), P(("tab", "rep"), None)),
        check_vma=False,
    )
```

profile of v0, /device:TPU:0, one launch (start us, length us, event | category | flops | bytes accessed | tf_op | source)
XLA Modules:
  0.0 536.2 jit_solution(541020844716352694)
XLA Ops:
  0.7 2.7 convolution_convert_fusion
  3.4 2.2 reshape.112
  5.6 7.5 %copy.20 = bf16[27,27,512]{1,0,2:T(8,128)(2,1)} copy(bf16[27,27,512]{2,1,0:T(8,128)(2,1)} %reshape.112) | data formatting | bytes 1492992 | tf_op jit(solution)/shard_map/reshape | solution.py:52
  13.1 4.5 fusion.25
  18.8 2.1 copy-done.2
  22.2 173.3 %while.25 = (s32[]{:T(128)}, bf16[26,1024,128]{2,1,0:T(8,128)(2,1)}, s32[26,1024]{1,0:T(8,128)}, s32[26,512]{1,0:T(8,128)}, bf16[26,512,128]{2,1,0:T(8,128)(2,1)S(1)}, /*index=5*/s32[]{:T(128)}, s32[]{:T(128)}) while((s32[]{:T(128)}, bf16[26,1024,128]{2,1,0:T(8,128)(2,1)}, s32[26,1024]{1,0:T(8,128)}, s32[26,512]{1,0:T(8,128)}, ...), condition=%wide.region_4.5_spmd, body=%wide.region_0.4_spmd.sunk | while | flops 143897568 | bytes 717545 | solution.py:69
  197.7 7.2 %all-to-all-start = ((s32[8,1,3328]{2,1,0:T(1,128)}), s32[8,1,3328]{2,1,0:T(1,128)S(1)}, u32[]{:S(2)}, u32[]{:S(2)}) async-start(s32[8,1,3328]{2,1,0:T(1,128)} %reshape.120), calls=%async_computation | async-start | bytes 212992 | tf_op jit(solution)/shard_map/all_to_all | solution.py:81
  205.0 8.6 %copy.26 = bf16[26,8,4,32,128]{4,3,2,0,1:T(8,128)(2,1)} copy(bf16[26,8,4,32,128]{4,3,2,1,0:T(8,128)(2,1)} %bitcast.88) | data formatting | bytes 13631488 | tf_op jit(solution)/shard_map/reshape | solution.py:70
  213.6 6.0 %all-to-all-start.2 = ((bf16[26,8,4,32,128]{4,3,2,0,1:T(8,128)(2,1)}), bf16[26,8,4,32,128]{4,3,2,0,1:T(8,128)(2,1)}, u32[]{:S(2)}, u32[]{:S(2)}) async-start(bf16[26,8,4,32,128]{4,3,2,0,1:T(8,128)(2,1)} %copy.26), calls=%async_computation.2 | async-start | bytes 13631488 | tf_op jit(solution)/shard_map/all_to_all | solution.py:74
  222.2 146.3 %all-to-all-done.2 = bf16[26,8,4,32,128]{4,3,2,0,1:T(8,128)(2,1)} async-done(((bf16[26,8,4,32,128]{4,3,2,0,1:T(8,128)(2,1)}), bf16[26,8,4,32,128]{4,3,2,0,1:T(8,128)(2,1)}, u32[]{:S(2)}, u32[]{:S(2)}) %all-to-all-start.2) | async-done | bytes 6815776 | tf_op jit(solution)/shard_map/all_to_all | solution.py:74
  368.5 3.5 all-to-all-start.1
  372.0 7.9 %copy.27 = bf16[26,8,4,32,128]{4,3,1,0,2:T(8,128)(2,1)} copy(bf16[26,8,4,32,128]{4,3,2,0,1:T(8,128)(2,1)} %all-to-all-done.2) | data formatting | bytes 13631488 | tf_op jit(solution)/shard_map/all_to_all | solution.py:74
  379.8 5.4 %all-to-all-start.3 = ((bf16[26,8,4,32,128]{4,3,1,0,2:T(8,128)(2,1)}), bf16[26,8,4,32,128]{4,3,1,0,2:T(8,128)(2,1)}, u32[]{:S(2)}, u32[]{:S(2)}) async-start(bf16[26,8,4,32,128]{4,3,1,0,2:T(8,128)(2,1)} %copy.27), calls=%async_computation.3 | async-start | bytes 13631488 | tf_op jit(solution)/shard_map/all_to_all | solution.py:73
  385.3 2.4 slice.25
  389.9 71.6 %all-to-all-done.3 = bf16[26,8,4,32,128]{4,3,1,0,2:T(8,128)(2,1)} async-done(((bf16[26,8,4,32,128]{4,3,1,0,2:T(8,128)(2,1)}), bf16[26,8,4,32,128]{4,3,1,0,2:T(8,128)(2,1)}, u32[]{:S(2)}, u32[]{:S(2)}) %all-to-all-start.3) | async-done | bytes 6815776 | tf_op jit(solution)/shard_map/all_to_all | solution.py:73
  461.6 8.0 %copy.28 = bf16[26,8,4,32,128]{4,3,2,1,0:T(8,128)(2,1)} copy(bf16[26,8,4,32,128]{4,3,1,0,2:T(8,128)(2,1)} %all-to-all-done.3) | data formatting | bytes 13631488 | tf_op jit(solution)/shard_map/all_to_all | solution.py:73
  469.6 66.7 %while.26 = (s32[]{:T(128)}, f32[26,128,128]{2,1,0:T(8,128)}, s32[26,1024]{1,0:T(8,128)}, bf16[26,1024,128]{2,1,0:T(8,128)(2,1)}, s32[]{:T(128)}) while((s32[]{:T(128)}, f32[26,128,128]{2,1,0:T(8,128)}, s32[26,1024]{1,0:T(8,128)}, bf16[26,1024,128]{2,1,0:T(8,128)(2,1)}, s32[]{:T(128)}) %tuple.59), condition=%wide.region_6.7_spmd, body=%wide.region_5.6_spmd.sunk | while | flops 33685504 | bytes 341065 | solution.py:43
  480.6 1.8 fusion.49
  483.1 1.8 fusion.49
  485.7 1.8 fusion.49
  501.1 1.8 fusion.49
  503.7 1.8 fusion.49
  521.6 1.8 fusion.49
  524.2 1.8 fusion.49
  (459 shorter events, 236.1 us)
Async XLA Ops:
  0.6 12.5 %copy-start = (bf16[512,27,128]{2,0,1:T(8,128)(2,1)S(1)}, bf16[512,27,128]{2,0,1:T(8,128)(2,1)}, u32[]{:S(2)}) copy-start(bf16[512,27,128]{2,0,1:T(8,128)(2,1)} %param.9) | copy-start | bytes 10616836
  17.7 3.2 copy-start.2
  197.7 15.9 %all-to-all-start = ((s32[8,1,3328]{2,1,0:T(1,128)}), s32[8,1,3328]{2,1,0:T(1,128)S(1)}, u32[]{:S(2)}, u32[]{:S(2)}) async-start(s32[8,1,3328]{2,1,0:T(1,128)} %reshape.120), calls=%async_computation | async-start | bytes 212992 | tf_op jit(solution)/shard_map/all_to_all | solution.py:81
  213.6 154.9 %all-to-all-start.2 = ((bf16[26,8,4,32,128]{4,3,2,0,1:T(8,128)(2,1)}), bf16[26,8,4,32,128]{4,3,2,0,1:T(8,128)(2,1)}, u32[]{:S(2)}, u32[]{:S(2)}) async-start(bf16[26,8,4,32,128]{4,3,2,0,1:T(8,128)(2,1)} %copy.26), calls=%async_computation.2 | async-start | bytes 13631488 | tf_op jit(solution)/shard_map/all_to_all | solution.py:74
  368.5 11.4 %all-to-all-start.1 = ((s32[4,1,6656]{2,1,0:T(1,128)}), s32[4,1,6656]{2,1,0:T(1,128)S(1)}, u32[]{:S(2)}, u32[]{:S(2)}) async-start(s32[4,1,6656]{2,1,0:T(1,128)} %reshape.122), calls=%async_computation.1 | async-start | bytes 212992 | tf_op jit(solution)/shard_map/all_to_all | solution.py:80
  379.8 81.7 %all-to-all-start.3 = ((bf16[26,8,4,32,128]{4,3,1,0,2:T(8,128)(2,1)}), bf16[26,8,4,32,128]{4,3,1,0,2:T(8,128)(2,1)}, u32[]{:S(2)}, u32[]{:S(2)}) async-start(bf16[26,8,4,32,128]{4,3,1,0,2:T(8,128)(2,1)} %copy.27), calls=%async_computation.3 | async-start | bytes 13631488 | tf_op jit(solution)/shard_map/all_to_all | solution.py:73
  461.5 74.7 %copy-start.1 = (bf16[512,27,128]{2,0,1:T(8,128)(2,1)S(1)}, bf16[512,27,128]{2,0,1:T(8,128)(2,1)}, u32[]{:S(2)}) copy-start(bf16[512,27,128]{2,0,1:T(8,128)(2,1)} %param.9) | copy-start | bytes 10616836
where the time goes:
time: 544 us; the launch traced here: 536 us
  waiting for transfers between devices  218 us (40%)
  local copies, waits for them, and re-layouts  128 us (24%)
  matrix products  111 us (20%)
  other arithmetic  56.4 us (10%)
  starting transfers between devices  22.1 us (4%)
    all_to_all x1, waiting for transfers between devices, local(): lax.all_to_all(outgoing, 'tab', split_axis=1, concat_axis=1, tiled=True)  146 us
    all_to_all x1, waiting for transfers between devices, local(): lax.all_to_all(lax.all_to_all(outgoing, 'tab', split_axis=1, concat_axis=...  71.6 us
    dot_general x26, matrix products, per_field(): return jnp.dot(matches, slot_grads, preferred_element_type=jnp.float32)  46.8 us
    dynamic_update_slice x26, local copies, waits for them, and re-layouts, local(): outgoing, row_tags = lax.map(build_owner, (ids_by_field, field_grads))  36.6 us
    another operation x52, other arithmetic  31.3 us
    dot_general x26, matrix products, place_field(): jnp.dot(placing.astype(jnp.bfloat16), grads, preferred_element_type=jnp.f...  30.5 us
    dot_general x26, matrix products, place_field(): jnp.dot(placing.astype(jnp.float32), shifted, precision=lax.Precision.HIG...  26.3 us
    dynamic_slice x26, local copies, waits for them, and re-layouts, tally_rows(): return lax.map(per_field, (arrived, row_tags))  19.9 us
  transfers between devices with their start and end apart: 4, of which 2 were waited for; matrix products, arithmetic and copies ran while one was open for 4% of the time, Pallas kernels for 0%

commit v1 on v0

v1 whole, which is shorter than its diff:
```python
import functools
import math

import jax
import jax.numpy as jnp
import numpy as np
from jax import lax
from jax.experimental import pallas as pl
from jax.experimental.pallas import tpu as pltpu
from jax.sharding import PartitionSpec as P

RQ = 128
LANES = 128
PACK = 16
SUB = 8


def pair_spread(vectors, width):
    row_of, col_of = np.tril_indices(vectors, -1)
    spread = np.zeros((row_of.shape[0], vectors, SUB, width), np.float32)
    places = np.arange(row_of.shape[0])
    spread[places, row_of, :, col_of] = 1.0
    spread[places, col_of, :, row_of] = 1.0
    return spread.reshape(row_of.shape[0], -1)


def meta_kernel(fields, owners, window, ids_ref, earlier_ref, below_ref, rank_ref, meta_ref, mine, before):
    samples = ids_ref.shape[1]
    last_base = samples - window
    owner_at = lax.broadcasted_iota(jnp.int32, (owners, samples), 0)
    for field in range(fields):
        own = ids_ref[field : field + 1, :] // RQ
        mine[field * owners : (field + 1) * owners, :] = jnp.where(owner_at == own, 1.0, 0.0).astype(jnp.bfloat16)
    before[...] = jnp.dot(mine[...], earlier_ref[...], preferred_element_type=jnp.float32)
    slot_at = lax.broadcasted_iota(jnp.int32, (LANES, samples), 0).astype(jnp.float32)
    lane = lax.broadcasted_iota(jnp.int32, (owners, LANES), 1)
    for field in range(fields):
        rows = slice(field * owners, (field + 1) * owners)
        hit = mine[rows, :].astype(jnp.float32)
        count = jnp.sum(hit, axis=1, keepdims=True)
        count = jnp.broadcast_to(count, (owners, LANES)).astype(jnp.bfloat16)
        start = jnp.dot(below_ref[...], count, preferred_element_type=jnp.float32)
        tile = jnp.minimum(jnp.floor(start * (1.0 / PACK)), float(last_base // PACK))
        start, tile_of = start[:, :1], tile[:, :1]
        place = before[rows, :] + start
        rank = jnp.sum(hit * place, axis=0, keepdims=True)
        slot = jnp.sum(hit * (place - tile_of * PACK), axis=0, keepdims=True)
        rank_ref[field : field + 1, :] = rank
        tag = (ids_ref[field : field + 1, :] % RQ + 1).astype(jnp.float32)
        tags = lax.dot_general(
            (hit * tag).astype(jnp.bfloat16),
            jnp.where(slot_at == slot, 1.0, 0.0).astype(jnp.bfloat16),
            (((1,), (1,)), ((), ())),
            preferred_element_type=jnp.float32,
        )
        meta_ref[field] = jnp.where(lane == LANES - 1, tile, tags).astype(jnp.bfloat16)
    for field in range(fields, meta_ref.shape[0]):
        meta_ref[field] = jnp.zeros((owners, LANES), jnp.bfloat16)


def grads_kernel(fields, pairs_ref, spread_ref, feat_ref, rank_ref, dense_ref, sorted_ref, weights, grads):
    samples, vectors, depth = feat_ref.shape
    span = spread_ref.shape[1] // vectors
    width = span // SUB
    own_lane = (
        lax.broadcasted_iota(jnp.int32, (SUB, span), 1) // width == lax.broadcasted_iota(jnp.int32, (SUB, span), 0)
    )
    own_lane = jnp.concatenate([own_lane.astype(jnp.float32)] * (samples // SUB), axis=0)
    for vector in range(vectors):
        spread_out = jnp.dot(
            pairs_ref[...], spread_ref[:, vector * span : (vector + 1) * span], preferred_element_type=jnp.float32
        )
        weights[:, vector] = (spread_out * own_lane).reshape(samples // SUB, SUB, span)

    def per_group(group, carry):
        first = pl.multiple_of(group * SUB, SUB)
        block = feat_ref[pl.ds(first, SUB)]
        block = jnp.concatenate([block, jnp.zeros((SUB, width - vectors, depth), block.dtype)], axis=1)
        left = weights[group].reshape(vectors * SUB, span).astype(jnp.bfloat16)
        out = jnp.dot(left, block.reshape(span, depth), preferred_element_type=jnp.float32)
        out = out.reshape(vectors, SUB, depth)
        dense_ref[pl.ds(first, SUB), :] = out[0]
        grads[:, pl.ds(first, SUB), :] = out[1:]
        return carry

    lax.fori_loop(0, samples // SUB, per_group, 0, unroll=2)
    slot_at = lax.broadcasted_iota(jnp.int32, (samples, samples), 0).astype(jnp.float32)

    def per_field(field, carry):
        placing = jnp.where(slot_at == rank_ref[pl.ds(field, 1), :], 1.0, 0.0).astype(jnp.bfloat16)
        placed = jnp.dot(placing, grads[field].astype(jnp.bfloat16), preferred_element_type=jnp.float32)
        sorted_ref[field] = placed.astype(jnp.bfloat16)
        return carry

    lax.fori_loop(0, fields, per_field, 0)


def tally_kernel(window, tile_ref, tags_ref, data_ref, out_ref):
    _, blocks, samples, depth = data_ref.shape
    owners = tags_ref.shape[1]
    field = pl.program_id(0)
    row_at = (lax.broadcasted_iota(jnp.int32, (RQ, blocks * window), 0) + 1).astype(jnp.float32)

    def per_owner(owner, carry):
        parts = []
        for block in range(blocks):
            tile = tile_ref[(field * owners + owner) * blocks + block]
            parts.append(data_ref[0, block, pl.ds(pl.multiple_of(tile * PACK, PACK), window), :])
        matches = jnp.where(row_at == tags_ref[0, pl.ds(owner, 1), :], 1.0, 0.0).astype(jnp.bfloat16)
        summed = jnp.dot(matches, jnp.concatenate(parts, axis=0), preferred_element_type=jnp.float32)
        out_ref[owner, 0] = summed.astype(jnp.bfloat16)
        return carry

    lax.fori_loop(0, owners, per_owner, 0, unroll=2)


def local(outer, inner, sample_ids, features, pair_grad):
    samples, vectors, depth = features.shape
    fields = vectors - 1
    owners = outer * inner
    capacity = 2 * samples // owners
    window = min(-(-(PACK - 1 + capacity) // PACK) * PACK, samples)
    per_device = -(-fields // inner)
    width = 2 * LANES // SUB
    vmem = pl.BlockSpec(memory_space=pltpu.VMEM)
    params = pltpu.CompilerParams(vmem_limit_bytes=60 * 2**20)

    order = np.arange(samples)
    earlier = jnp.asarray(order[:, None] < order[None, :]).astype(jnp.bfloat16)
    below = jnp.asarray(np.arange(owners)[:, None] > np.arange(owners)[None, :]).astype(jnp.bfloat16)
    rank, meta = pl.pallas_call(
        functools.partial(meta_kernel, fields, owners, window),
        out_shape=(
            jax.ShapeDtypeStruct((fields, samples), jnp.float32),
            jax.ShapeDtypeStruct((per_device * inner, owners, LANES), jnp.bfloat16),
        ),
        in_specs=[vmem] * 3,
        out_specs=[vmem] * 2,
        scratch_shapes=[
            pltpu.VMEM((fields * owners, samples), jnp.bfloat16),
            pltpu.VMEM((fields * owners, samples), jnp.float32),
        ],
        compiler_params=params,
        name="meta",
    )(sample_ids.T, earlier, below)
    every = ("tab", "rep")
    groups = [list(range(first, first + inner)) for first in range(0, owners, inner)]
    exchange = functools.partial(
        lax.all_to_all, axis_name=every, split_axis=1, concat_axis=1, tiled=True, axis_index_groups=groups
    )
    meta = exchange(meta.reshape(per_device, inner, owners, LANES))
    tiles = meta[..., LANES - 1].astype(jnp.int32).transpose(0, 2, 1).reshape(-1)
    tags = meta[..., :window].transpose(0, 2, 1, 3).reshape(per_device, owners, inner * window).astype(jnp.float32)

    spread = jnp.asarray(pair_spread(vectors, width)).astype(jnp.bfloat16)
    dense_grad, in_order = pl.pallas_call(
        functools.partial(grads_kernel, fields),
        out_shape=(
            jax.ShapeDtypeStruct((samples, depth), jnp.float32),
            jax.ShapeDtypeStruct((per_device * inner, samples, depth), jnp.bfloat16),
        ),
        in_specs=[vmem] * 4,
        out_specs=[vmem] * 2,
        scratch_shapes=[
            pltpu.VMEM((samples // SUB, vectors, SUB, SUB * width), jnp.float32),
            pltpu.VMEM((fields, samples, depth), jnp.float32),
        ],
        compiler_params=params,
        name="grads",
    )(pair_grad.T, spread, features, rank)
    arrived = exchange(in_order.reshape(per_device, inner, samples, depth))
    partial_rows = pl.pallas_call(
        functools.partial(tally_kernel, window),
        out_shape=jax.ShapeDtypeStruct((owners, per_device, RQ, depth), jnp.bfloat16),
        grid_spec=pltpu.PrefetchScalarGridSpec(
            num_scalar_prefetch=1,
            grid=(per_device,),
            in_specs=[
                pl.BlockSpec((1, owners, inner * window), lambda f, _: (f, 0, 0)),
                pl.BlockSpec((1, inner, samples, depth), lambda f, _: (f, 0, 0, 0)),
            ],
            out_specs=pl.BlockSpec((owners, 1, RQ, depth), lambda f, _: (0, f, 0, 0)),
        ),
        compiler_params=params,
        name="tally",
    )(tiles, tags, arrived)
    rows = lax.all_to_all(partial_rows, every, split_axis=0, concat_axis=0, tiled=True)
    rows = rows.reshape(outer, inner, per_device, RQ, depth).astype(jnp.float32).sum(axis=0)
    table_grad = rows.transpose(1, 0, 2, 3).reshape(per_device * inner, RQ, depth)[:fields]
    return table_grad, dense_grad


def solution(mesh):
    tab, rep = mesh.shape["tab"], mesh.shape["rep"]
    inner = rep * math.gcd(tab, 4)
    every = ("tab", "rep")
    return jax.shard_map(
        functools.partial(local, tab * rep // inner, inner),
        mesh=mesh,
        in_specs=(P(every, None), P(every, None, None), P(None, every)),
        out_specs=(P(None, every, None), P(every, None)),
        check_vma=False,
    )
```

time: 544 us -> 191 us (0.35); the launches traced: 536 us -> 190 us
  waiting for transfers between devices: 218 us -> 56.8 us
  matrix products: 111 us -> 0 us
  local copies, waits for them, and re-layouts: 128 us -> 23 us
  other arithmetic: 56.4 us -> 0.51 us
  blocking collectives: 0 us -> 55.4 us
  Pallas kernels: 0 us -> 42.4 us
  starting transfers between devices: 22.1 us -> 11.5 us
    all_to_all x4 -> x2, waiting for transfers between devices: 218 us -> 56.8 us  [the longest x1 56.8 us: local(): arrived = exchange(in_order.reshape(per_device, inner, samples, depth))]
    dot_general x80 -> x0, matrix products: 111 us -> none  [the longest x26 46.8 us: per_field(): return jnp.dot(matches, slot_grads, preferred_element_type=jnp.float32)]
    all_to_all x0 -> x1, blocking collectives: none -> 55.4 us  [local(): lax.all_to_all(partial_rows, every, split_axis=0, concat_axis=0, tiled=True)]
    pallas_call x0 -> x3, Pallas kernels: none -> 42.4 us  [the longest x1 24.1 us: local(): pl.pallas_call(functools.partial(grads_kernel, fields), out_shape=(jax.Sh...]
    dynamic_slice x52 -> x0, local copies, waits for them, and re-layouts: 38.6 us -> none  [the longest x26 19.9 us: tally_rows(): return lax.map(per_field, (arrived, row_tags))]
    dynamic_update_slice x26 -> x0, local copies, waits for them, and re-layouts: 36.6 us -> none  [local(): outgoing, row_tags = lax.map(build_owner, (ids_by_field, field_grads))]
    another operation x52 -> x0, other arithmetic: 31.3 us -> none
    add x26 -> x0, other arithmetic: 19.3 us -> none  [build_owner(): slot_of = owners * capacity + arrival_order(owners, col_count * rep_count)]
  transfers between devices with their start and end apart: 4 -> 2, of which waited for: 2 -> 1; matrix products, arithmetic and copies ran while one was open for 4% -> 8% of each run, Pallas kernels for 0% -> 13%
where the time goes in v1:
time: 191 us; the launch traced here: 190 us
  waiting for transfers between devices  56.8 us (30%)
  blocking collectives  55.4 us (29%)
  Pallas kernels  42.4 us (22%)
  local copies, waits for them, and re-layouts  23 us (12%)
  starting transfers between devices  11.5 us (6%)
    all_to_all x1, waiting for transfers between devices, local(): arrived = exchange(in_order.reshape(per_device, inner, samples, depth))  56.8 us
    all_to_all x1, blocking collectives, local(): lax.all_to_all(partial_rows, every, split_axis=0, concat_axis=0, tiled=True)  55.4 us
    pallas_call x1, Pallas kernels, local(): pl.pallas_call(functools.partial(grads_kernel, fields), out_shape=(jax.Sh...  24.1 us
    pallas_call x1, Pallas kernels, local(): pl.pallas_call(functools.partial(tally_kernel, window), out_shape=jax.Sha...  11.9 us
    unnamed x3, local copies, waits for them, and re-layouts  8.47 us
    pallas_call x1, Pallas kernels, local(): pl.pallas_call(functools.partial(meta_kernel, fields, owners, window), ou...  6.5 us
    all_to_all x1, starting transfers between devices, local(): meta = exchange(meta.reshape(per_device, inner, owners, LANES))  6.32 us
    all_to_all x1, starting transfers between devices, local(): arrived = exchange(in_order.reshape(per_device, inner, samples, depth))  5.16 us
  transfers between devices with their start and end apart: 2, of which 1 were waited for; matrix products, arithmetic and copies ran while one was open for 8% of the time, Pallas kernels for 13%

profile of v1, /device:TPU:0, one launch (start us, length us, event | category | flops | bytes accessed | tf_op | source)
XLA Modules:
  0.0 190.3 jit_solution(14510910895011875079)
XLA Ops:
  0.6 6.5 %meta.1 = (f32[26,512]{1,0:T(8,128)}, bf16[32,32,128]{2,1,0:T(8,128)(2,1)}) custom-call(s32[26,512]{1,0:T(8,128)} %bitcast.23, bf16[512,512]{1,0:T(8,128)(2,1)} %constant.11.earlier_ref, bf16[32,32]{1,0:T(8,128)(2,1)} %constant.12.below_ref), custom_call_target="tpu_custom_call" | custom-call | tf_op jit(solution)/shard_map/meta/pallas_call | solution.py:131
  7.1 1.7 copy.24
  8.8 6.3 %all-to-all-start = ((bf16[2,16,32,128]{3,2,0,1:T(8,128)(2,1)}), bf16[2,16,32,128]{3,2,0,1:T(8,128)(2,1)S(1)}, u32[]{:S(2)}, u32[]{:S(2)}) async-start(bf16[2,16,32,128]{3,2,0,1:T(8,128)(2,1)} %copy.24), calls=%async_computation | async-start | bytes 524288 | tf_op jit(solution)/shard_map/all_to_all | solution.py:151
  15.2 1.9 %copy.28 = bf16[351,512]{0,1:T(8,128)(2,1)} copy(bf16[351,512]{1,0:T(8,128)(2,1)} %param.8) | data formatting | bytes 718848 | tf_op args[2]
  17.1 6.3 %copy.29.feat_ref = bf16[512,27,128]{2,1,0:T(8,128)(2,1)} copy(bf16[512,27,128]{2,0,1:T(8,128)(2,1)} %param.7) | data formatting | bytes 7077888 | tf_op args[1]
  23.4 24.1 %grads.1 = (f32[512,128]{1,0:T(8,128)}, bf16[32,512,128]{2,1,0:T(8,128)(2,1)}) custom-call(bf16[512,351]{1,0:T(8,128)(2,1)} %bitcast.21, bf16[351,6912]{1,0:T(8,128)(2,1)} %constant.13.spread_ref, bf16[512,27,128]{2,1,0:T(8,128)(2,1)} %copy.29.feat_ref, f32[26,512]{1,0:T(8,128)} %get-tuple-element.7.rank_ref), custom_call_target="tpu_custom_call" | custom-call | tf_op jit(solution)/shard_map/grads/pallas_call | solution.py:156
  47.4 4.6 %copy.30 = bf16[2,16,512,128]{3,2,0,1:T(8,128)(2,1)} copy(bf16[2,16,512,128]{3,2,1,0:T(8,128)(2,1)} %bitcast.20) | data formatting | bytes 8388608 | tf_op jit(solution)/shard_map/reshape | solution.py:171
  52.0 0.0 all-to-all-done
  52.0 5.2 %all-to-all-start.1 = ((bf16[2,16,512,128]{3,2,0,1:T(8,128)(2,1)}), bf16[2,16,512,128]{3,2,0,1:T(8,128)(2,1)}, u32[]{:S(2)}, u32[]{:S(2)}) async-start(bf16[2,16,512,128]{3,2,0,1:T(8,128)(2,1)} %copy.30), calls=%async_computation.1 | async-start | bytes 8388608 | tf_op jit(solution)/shard_map/all_to_all | solution.py:171
  57.2 0.1 slice.12
  57.3 0.3 copy.33
  57.6 0.1 copy.26
  57.7 0.7 reshape.32.tile_ref
  58.4 0.3 copy.27
  58.7 0.9 reshape.33.tags_ref
  59.6 56.8 %all-to-all-done.1 = bf16[2,16,512,128]{3,2,0,1:T(8,128)(2,1)} async-done(((bf16[2,16,512,128]{3,2,0,1:T(8,128)(2,1)}), bf16[2,16,512,128]{3,2,0,1:T(8,128)(2,1)}, u32[]{:S(2)}, u32[]{:S(2)}) %all-to-all-start.1) | async-done | bytes 4194336 | tf_op jit(solution)/shard_map/all_to_all | solution.py:171
  116.4 4.6 %copy.31.data_ref = bf16[2,16,512,128]{3,2,1,0:T(8,128)(2,1)} copy(bf16[2,16,512,128]{3,2,0,1:T(8,128)(2,1)} %all-to-all-done.1) | data formatting | bytes 8388608 | tf_op jit(solution)/shard_map/all_to_all | solution.py:171
  121.0 11.9 %tally.1 = bf16[32,2,128,128]{3,2,1,0:T(8,128)(2,1)} custom-call(s32[1024]{0:T(1024)} %reshape.32.tile_ref, f32[2,32,768]{2,1,0:T(8,128)} %reshape.33.tags_ref, bf16[2,16,512,128]{3,2,1,0:T(8,128)(2,1)} %copy.31.data_ref), custom_call_target="tpu_custom_call" | custom-call | tf_op jit(solution)/shard_map/tally/pallas_call | solution.py:172
  132.9 55.4 %all_to_all.15 = bf16[32,2,128,128]{3,2,1,0:T(8,128)(2,1)S(1)} all-to-all(bf16[32,2,128,128]{3,2,1,0:T(8,128)(2,1)} %tally.1), channel_id=1, replica_groups=mesh['tab'=8,'rep'=4] {'tab','rep'}, dimensions={0} | all-to-all | bytes 4194304 | tf_op jit(solution)/shard_map/all_to_all | solution.py:187
  188.3 0.5 convert_reduce_fusion
  188.8 0.2 copy.32
  189.0 1.3 slice.14
  (2 shorter events, 0.1 us)
Async XLA Ops:
  8.8 43.2 %all-to-all-start = ((bf16[2,16,32,128]{3,2,0,1:T(8,128)(2,1)}), bf16[2,16,32,128]{3,2,0,1:T(8,128)(2,1)S(1)}, u32[]{:S(2)}, u32[]{:S(2)}) async-start(bf16[2,16,32,128]{3,2,0,1:T(8,128)(2,1)} %copy.24), calls=%async_computation | async-start | bytes 524288 | tf_op jit(solution)/shard_map/all_to_all | solution.py:151
  52.0 64.4 %all-to-all-start.1 = ((bf16[2,16,512,128]{3,2,0,1:T(8,128)(2,1)}), bf16[2,16,512,128]{3,2,0,1:T(8,128)(2,1)}, u32[]{:S(2)}, u32[]{:S(2)}) async-start(bf16[2,16,512,128]{3,2,0,1:T(8,128)(2,1)} %copy.30), calls=%async_computation.1 | async-start | bytes 8388608 | tf_op jit(solution)/shard_map/all_to_all | solution.py:171

commit v2 on v0

v2 whole, which is shorter than its diff:
```python
import functools
import math

import jax
import jax.numpy as jnp
from jax import lax
from jax.experimental import pallas as pl
from jax.experimental.pallas import tpu as pltpu
from jax.sharding import PartitionSpec as P

RQ = 128
LANES = 128
PACK = 16
SUB = 8
HALVES = 2


def iota(shape, dim):
    return lax.broadcasted_iota(jnp.int32, shape, dim)


def one_hot(hit):
    return jnp.where(hit, 1.0, 0.0).astype(jnp.bfloat16)


def order_fields(first, count, owners, window, ids_ref, payload_ref, rank_ref, mine):
    samples = ids_ref.shape[1]
    pitch = LANES // HALVES
    last_tile = (samples - window) // PACK
    for at in range(count):
        own = ids_ref[first + at : first + at + 1, :] // RQ
        mine[at * owners : (at + 1) * owners, :] = one_hot(iota((owners, samples), 0) == own)
    earlier = one_hot(iota((samples, samples), 0) < iota((samples, samples), 1))
    before = jnp.dot(mine[...], earlier, preferred_element_type=jnp.float32)
    held = jnp.dot(mine[...], jnp.ones((samples, LANES), jnp.bfloat16), preferred_element_type=jnp.float32)
    below = one_hot(iota((owners, owners), 0) > iota((owners, owners), 1))
    slot_at = iota((LANES, samples), 0).astype(jnp.float32)
    lane = iota((owners // HALVES, LANES), 1)
    for at in range(count):
        rows = slice(at * owners, (at + 1) * owners)
        start = jnp.dot(below, held[rows].astype(jnp.bfloat16), preferred_element_type=jnp.float32)
        tile = jnp.minimum(jnp.floor(start * (1.0 / PACK)), float(last_tile))
        hit = mine[rows, :].astype(jnp.float32)
        place = hit * (before[rows] + jnp.concatenate([start] * (samples // LANES), axis=1))
        base = hit * jnp.concatenate([tile * PACK] * (samples // LANES), axis=1)
        rank = jnp.sum(place, axis=0, keepdims=True)
        slot = rank - jnp.sum(base, axis=0, keepdims=True)
        rank_ref[at : at + 1, :] = rank
        tag = (ids_ref[first + at : first + at + 1, :] % RQ + 1).astype(jnp.float32)
        tags = lax.dot_general(
            (hit * tag).astype(jnp.bfloat16),
            one_hot(slot_at == slot),
            (((1,), (1,)), ((), ())),
            preferred_element_type=jnp.float32,
        )
        half = owners // HALVES
        row = tags[:half] + pltpu.roll(tags[half:], pitch, 1)
        row = jnp.where(lane == pitch - 1, tile[:half], jnp.where(lane == LANES - 1, tile[half:], row))
        payload_ref[at, samples:, :] = row.astype(jnp.bfloat16)


def send_kernel(first, count, dense, owners, window, ids_ref, pairs_ref, feat_ref, *rest):
    if dense:
        dense_ref, payload_ref, rank_ref, mine, weights, grads = rest
    else:
        payload_ref, rank_ref, mine, weights, grads = rest
    vectors, samples, depth = feat_ref.shape
    span = 2 * LANES
    order_fields(first, count, owners, window, ids_ref, payload_ref, rank_ref, mine)
    for at in range(count, payload_ref.shape[0]):
        payload_ref[at] = jnp.zeros(payload_ref.shape[1:], jnp.bfloat16)

    targets = ([0] if dense else []) + list(range(first + 1, first + 1 + count))
    pairs = pairs_ref[...].astype(jnp.float32).T.astype(jnp.bfloat16)
    pair_at = iota((pairs.shape[1], span), 0)
    source = iota((1, span), 1) // SUB
    own_lane = one_hot(iota((PACK, span), 1) % SUB == iota((PACK, span), 0) % SUB)

    def spread_of(target):
        pair = jnp.where(source < target, target * (target - 1) // 2 + source, source * (source - 1) // 2 + target)
        pair = jnp.where((source == target) | (source >= vectors), -1, pair)
        found = jnp.dot(pairs, one_hot(pair_at == pair), preferred_element_type=jnp.float32)
        return found.reshape(samples // SUB, SUB, span)

    for at in range(0, len(targets), 2):
        low = spread_of(targets[at])
        high = spread_of(targets[at + 1]) if at + 1 < len(targets) else jnp.zeros_like(low)
        weights[:, at // 2] = jnp.concatenate([low, high], axis=1).astype(jnp.bfloat16) * own_lane

    def per_group(group, carry):
        begin = pl.multiple_of(group * PACK, PACK)
        block = feat_ref[:, pl.ds(begin, PACK), :].astype(jnp.float32)
        outs = []
        for part in range(PACK // SUB):
            right = block[:, part * SUB : (part + 1) * SUB, :].reshape(vectors * SUB, depth)
            right = jnp.concatenate([right, jnp.zeros((span - vectors * SUB, depth), jnp.float32)], axis=0)
            left = weights[group * (PACK // SUB) + part].reshape(-1, span)
            out = jnp.dot(left, right.astype(jnp.bfloat16), preferred_element_type=jnp.float32)
            outs.append(out.reshape(-1, SUB, depth))
        out = jnp.concatenate(outs, axis=1)
        if dense:
            dense_ref[pl.ds(begin, PACK), :] = out[0]
            out = out[1:]
        grads[:, pl.ds(begin, PACK), :] = out[:count].astype(jnp.bfloat16)
        return carry

    lax.fori_loop(0, samples // PACK, per_group, 0, unroll=2)
    slot_at = iota((samples, samples), 0).astype(jnp.float32)

    def per_field(at, carry):
        placing = one_hot(slot_at == rank_ref[pl.ds(at, 1), :])
        placed = jnp.dot(placing, grads[at], preferred_element_type=jnp.float32)
        payload_ref[at, :samples, :] = placed.astype(jnp.bfloat16)
        return carry

    lax.fori_loop(0, count, per_field, 0, unroll=2)


def tally_kernel(window, samples, data_ref, out_ref, tags, tiles, tile_at, done):
    blocks = data_ref.shape[0]
    owners = out_ref.shape[0]
    half, pitch = owners // HALVES, LANES // HALVES
    lane = iota((half, LANES), 1)
    tags[...] = jnp.zeros_like(tags)
    found = jnp.zeros((half, LANES), jnp.float32)
    for block in range(blocks):
        rows = data_ref[block, samples:, :].astype(jnp.float32)
        column, offset = divmod(block * window, LANES)
        for part in range(HALVES):
            own = slice(part * half, (part + 1) * half)
            tile_lane = part * blocks + block
            found = jnp.where(
                lane == tile_lane, pltpu.roll(rows, (tile_lane - (part * pitch + pitch - 1)) % LANES, 1), found
            )
            shifted = pltpu.roll(rows, (offset - part * pitch) % LANES, 1) if offset != part * pitch else rows
            fits = min(window, LANES - offset)
            here = slice(column * LANES, (column + 1) * LANES)
            tags[own, here] = jnp.where((lane >= offset) & (lane < offset + fits), shifted, tags[own, here])
            if fits < window:
                after = slice((column + 1) * LANES, (column + 2) * LANES)
                tags[own, after] = jnp.where(lane < window - fits, shifted, tags[own, after])
    tiles[...] = found.astype(jnp.int32)
    copy = pltpu.make_async_copy(tiles, tile_at, done)
    copy.start()
    copy.wait()
    row_at = (iota((RQ, blocks * window), 0) + 1).astype(jnp.float32)

    def per_owner(owner, carry):
        part, row = owner // half, owner % half
        picked = []
        for block in range(blocks):
            tile = tile_at[row, part * blocks + block]
            picked.append(data_ref[block, pl.ds(pl.multiple_of(tile * PACK, PACK), window), :])
        matches = one_hot(row_at == tags[pl.ds(owner, 1), : blocks * window])
        summed = jnp.dot(matches, jnp.concatenate(picked, axis=0), preferred_element_type=jnp.float32)
        out_ref[owner] = summed.astype(jnp.bfloat16)
        return carry

    lax.fori_loop(0, owners, per_owner, 0, unroll=4)


def local(outer, inner, sample_ids, features, pair_grad):
    samples, vectors, depth = features.shape
    fields = vectors - 1
    owners = outer * inner
    capacity = 2 * samples // owners
    window = min(-(-(PACK - 1 + capacity) // PACK) * PACK, samples)
    extra = owners // HALVES
    every = ("tab", "rep")
    groups = [list(range(start, start + inner)) for start in range(0, owners, inner)]
    vmem = pl.BlockSpec(memory_space=pltpu.VMEM)
    params = pltpu.CompilerParams(vmem_limit_bytes=60 * 2**20)
    ids = sample_ids.T
    by_vector = features.transpose(1, 0, 2)

    def send(first, count, dense):
        targets = count + dense
        shapes = [jax.ShapeDtypeStruct((inner, samples + extra, depth), jnp.bfloat16)]
        if dense:
            shapes = [jax.ShapeDtypeStruct((samples, depth), jnp.float32)] + shapes
        return pl.pallas_call(
            functools.partial(send_kernel, first, count, dense, owners, window),
            out_shape=shapes,
            in_specs=[vmem] * 3,
            out_specs=[vmem] * len(shapes),
            scratch_shapes=[
                pltpu.VMEM((count, samples), jnp.float32),
                pltpu.VMEM((count * owners, samples), jnp.bfloat16),
                pltpu.VMEM((samples // SUB, -(-targets // 2), PACK, 2 * LANES), jnp.bfloat16),
                pltpu.VMEM((count, samples, depth), jnp.bfloat16),
            ],
            cost_estimate=pl.CostEstimate(
                flops=2 * targets * samples * samples * depth, bytes_accessed=2 * features.size, transcendentals=0
            ),
            compiler_params=params,
            name="send",
        )(ids, pair_grad, by_vector)

    def tally(arrived):
        return pl.pallas_call(
            functools.partial(tally_kernel, window, samples),
            out_shape=jax.ShapeDtypeStruct((owners, RQ, depth), jnp.bfloat16),
            in_specs=[vmem],
            out_specs=vmem,
            scratch_shapes=[
                pltpu.VMEM((owners, -(-inner * window // LANES) * LANES), jnp.float32),
                pltpu.VMEM((extra, LANES), jnp.int32),
                pltpu.SMEM((extra, LANES), jnp.int32),
                pltpu.SemaphoreType.DMA,
            ],
            cost_estimate=pl.CostEstimate(
                flops=2 * owners * inner * window * RQ * depth, bytes_accessed=2 * arrived.size, transcendentals=0
            ),
            compiler_params=params,
            name="tally",
        )(arrived)

    firsts = list(range(0, fields, inner))
    outgoing = []
    for first in firsts:
        outgoing.append(send(first, min(inner, fields - first), first == firsts[-1]))
    dense_grad = outgoing[-1][0]
    tables = []
    for first, sent in zip(firsts, outgoing):
        arrived = lax.all_to_all(
            sent[-1], every, split_axis=0, concat_axis=0, tiled=True, axis_index_groups=groups
        )
        rows = lax.all_to_all(tally(arrived), every, split_axis=0, concat_axis=0, tiled=True)
        rows = rows.reshape(outer, inner, RQ, depth)[:, : min(inner, fields - first)]
        tables.append(rows.astype(jnp.float32).sum(axis=0))
    return jnp.concatenate(tables, axis=0), dense_grad


def solution(mesh):
    tab, rep = mesh.shape["tab"], mesh.shape["rep"]
    inner = rep * math.gcd(tab, 4)
    every = ("tab", "rep")
    return jax.shard_map(
        functools.partial(local, tab * rep // inner, inner),
        mesh=mesh,
        in_specs=(P(every, None), P(every, None, None), P(None, every)),
        out_specs=(P(None, every, None), P(every, None)),
        check_vma=False,
    )
```

time: 544 us -> 149 us (0.27); the launches traced: 536 us -> 148 us
  waiting for transfers between devices: 218 us -> 84 us
  local copies, waits for them, and re-layouts: 128 us -> 1.34 us
  matrix products: 111 us -> 0 us
  other arithmetic: 56.4 us -> 1.6 us
  Pallas kernels: 0 us -> 42.2 us
    all_to_all x4, waiting for transfers between devices: 218 us -> 84 us  [the longest x2 45.5 us: local(): lax.all_to_all(tally(arrived), every, split_axis=0, concat_axis=0, tiled=...]
    dot_general x80 -> x0, matrix products: 111 us -> none  [the longest x26 46.8 us: per_field(): return jnp.dot(matches, slot_grads, preferred_element_type=jnp.float32)]
    pallas_call x0 -> x4, Pallas kernels: none -> 42.2 us  [the longest x2 28.6 us: send(): pl.pallas_call(functools.partial(send_kernel, first, count, dense, owners...]
    dynamic_slice x52 -> x0, local copies, waits for them, and re-layouts: 38.6 us -> none  [the longest x26 19.9 us: tally_rows(): return lax.map(per_field, (arrived, row_tags))]
    dynamic_update_slice x26 -> x0, local copies, waits for them, and re-layouts: 36.6 us -> none  [local(): outgoing, row_tags = lax.map(build_owner, (ids_by_field, field_grads))]
    another operation x52 -> x0, other arithmetic: 31.3 us -> none
    reshape x6 -> x0, local copies, waits for them, and re-layouts: 20.6 us -> none  [the longest x2 9.73 us: local(): symmetric.astype(jnp.bfloat16).reshape(vectors, vectors, samples)]
    add x26 -> x0, other arithmetic: 19.3 us -> none  [build_owner(): slot_of = owners * capacity + arrival_order(owners, col_count * rep_count)]
  transfers between devices with their start and end apart: 4 -> 4, of which waited for: 2 -> 4; matrix products, arithmetic and copies ran while one was open for 4% -> 0% of each run, Pallas kernels for 0% -> 9%
where the time goes in v2:
time: 149 us; the launch traced here: 148 us
  waiting for transfers between devices  84 us (56%)
  Pallas kernels  42.2 us (28%)
  starting transfers between devices  18.3 us (12%)
  other arithmetic  1.6 us (1%)
    all_to_all x2, waiting for transfers between devices, local(): lax.all_to_all(tally(arrived), every, split_axis=0, concat_axis=0, tiled=...  45.5 us
    all_to_all x2, waiting for transfers between devices, local(): lax.all_to_all(sent[-1], every, split_axis=0, concat_axis=0, tiled=True,...  38.5 us
    pallas_call x2, Pallas kernels, send(): pl.pallas_call(functools.partial(send_kernel, first, count, dense, owners...  28.6 us
    pallas_call x2, Pallas kernels, tally(): pl.pallas_call(functools.partial(tally_kernel, window, samples), out_shap...  13.6 us
    all_to_all x2, starting transfers between devices, local(): lax.all_to_all(sent[-1], every, split_axis=0, concat_axis=0, tiled=True,...  10 us
    all_to_all x2, starting transfers between devices, local(): lax.all_to_all(tally(arrived), every, split_axis=0, concat_axis=0, tiled=...  8.23 us
  transfers between devices with their start and end apart: 4, of which 4 were waited for; matrix products, arithmetic and copies ran while one was open for 0% of the time, Pallas kernels for 9%

profile of v2, /device:TPU:0, one launch (start us, length us, event | category | flops | bytes accessed | tf_op | source)
XLA Modules:
  0.0 148.0 jit_solution(5499144105598880133)
XLA Ops:
  0.6 12.7 %send.3 = (f32[512,128]{1,0:T(8,128)}, bf16[16,528,128]{2,1,0:T(8,128)(2,1)}) custom-call(s32[26,512]{1,0:T(8,128)} %bitcast.9, bf16[351,512]{1,0:T(8,128)(2,1)} %pairs_ref.3, bf16[27,512,128]{2,1,0:T(8,128)(2,1)} %bitcast.5), custom_call_target="tpu_custom_call" | custom-call | flops 738197504 | bytes 3538944 | tf_op jit(solution)/shard_map/send/pallas_call | solution.py:181
  13.3 6.3 %all-to-all-start.2 = ((bf16[16,528,128]{2,1,0:T(8,128)(2,1)}), bf16[16,528,128]{2,1,0:T(8,128)(2,1)S(1)}, u32[]{:S(2)}, u32[]{:S(2)}) async-start(bf16[16,528,128]{2,1,0:T(8,128)(2,1)} %get-tuple-element.4), calls=%async_computation.2 | async-start | bytes 4325376 | tf_op jit(solution)/shard_map/all_to_all | solution.py:225
  19.6 15.9 %send.2 = bf16[16,528,128]{2,1,0:T(8,128)(2,1)} custom-call(s32[26,512]{1,0:T(8,128)} %bitcast.10, bf16[351,512]{1,0:T(8,128)(2,1)} %pairs_ref.3, bf16[27,512,128]{2,1,0:T(8,128)(2,1)} %bitcast.6), custom_call_target="tpu_custom_call" | custom-call | flops 1073741824 | bytes 3538944 | tf_op jit(solution)/shard_map/send/pallas_call | solution.py:181
  35.5 14.7 %all-to-all-done.2.data_ref = bf16[16,528,128]{2,1,0:T(8,128)(2,1)S(1)} async-done(((bf16[16,528,128]{2,1,0:T(8,128)(2,1)}), bf16[16,528,128]{2,1,0:T(8,128)(2,1)S(1)}, u32[]{:S(2)}, u32[]{:S(2)}) %all-to-all-start.2) | async-done | bytes 2162720 | tf_op jit(solution)/shard_map/all_to_all | solution.py:225
  50.2 0.0 copy-start.1
  50.2 1.3 copy-done.1
  51.6 3.7 %all-to-all-start = ((bf16[16,528,128]{2,1,0:T(8,128)(2,1)}), bf16[16,528,128]{2,1,0:T(8,128)(2,1)S(1)}, u32[]{:S(2)}, u32[]{:S(2)}) async-start(bf16[16,528,128]{2,1,0:T(8,128)(2,1)} %send.2), calls=%async_computation | async-start | bytes 4325376 | tf_op jit(solution)/shard_map/all_to_all | solution.py:225
  55.3 6.8 %tally.3 = bf16[32,128,128]{2,1,0:T(8,128)(2,1)} custom-call(bf16[16,528,128]{2,1,0:T(8,128)(2,1)} %copy-done.1), custom_call_target="tpu_custom_call" | custom-call | flops 805306368 | bytes 2162688 | tf_op jit(solution)/shard_map/tally/pallas_call | solution.py:200
  62.1 23.8 %all-to-all-done.data_ref = bf16[16,528,128]{2,1,0:T(8,128)(2,1)S(1)} async-done(((bf16[16,528,128]{2,1,0:T(8,128)(2,1)}), bf16[16,528,128]{2,1,0:T(8,128)(2,1)S(1)}, u32[]{:S(2)}, u32[]{:S(2)}) %all-to-all-start) | async-done | bytes 2162720 | tf_op jit(solution)/shard_map/all_to_all | solution.py:225
  85.9 0.0 copy-start
  85.9 4.6 %all-to-all-start.3 = ((bf16[32,128,128]{2,1,0:T(8,128)(2,1)}), bf16[32,128,128]{2,1,0:T(8,128)(2,1)S(1)}, u32[]{:S(2)}, u32[]{:S(2)}) async-start(bf16[32,128,128]{2,1,0:T(8,128)(2,1)} %tally.3), calls=%async_computation.3 | async-start | bytes 2097152 | tf_op jit(solution)/shard_map/all_to_all | solution.py:228
  90.5 0.0 copy-done
  90.5 6.8 %tally.2 = bf16[32,128,128]{2,1,0:T(8,128)(2,1)} custom-call(bf16[16,528,128]{2,1,0:T(8,128)(2,1)} %copy-done), custom_call_target="tpu_custom_call" | custom-call | flops 805306368 | bytes 2162688 | tf_op jit(solution)/shard_map/tally/pallas_call | solution.py:200
  97.3 19.4 %all-to-all-done.3 = bf16[32,128,128]{2,1,0:T(8,128)(2,1)S(1)} async-done(((bf16[32,128,128]{2,1,0:T(8,128)(2,1)}), bf16[32,128,128]{2,1,0:T(8,128)(2,1)S(1)}, u32[]{:S(2)}, u32[]{:S(2)}) %all-to-all-start.3) | async-done | bytes 1048608 | tf_op jit(solution)/shard_map/all_to_all | solution.py:228
  116.7 3.6 %all-to-all-start.1 = ((bf16[32,128,128]{2,1,0:T(8,128)(2,1)}), bf16[32,128,128]{2,1,0:T(8,128)(2,1)S(1)}, u32[]{:S(2)}, u32[]{:S(2)}) async-start(bf16[32,128,128]{2,1,0:T(8,128)(2,1)} %tally.2), calls=%async_computation.1 | async-start | bytes 2097152 | tf_op jit(solution)/shard_map/all_to_all | solution.py:228
  120.3 0.1 convert_reduce_fusion.1
  120.5 26.1 %all-to-all-done.1 = bf16[32,128,128]{2,1,0:T(8,128)(2,1)S(1)} async-done(((bf16[32,128,128]{2,1,0:T(8,128)(2,1)}), bf16[32,128,128]{2,1,0:T(8,128)(2,1)S(1)}, u32[]{:S(2)}, u32[]{:S(2)}) %all-to-all-start.1) | async-done | bytes 1048608 | tf_op jit(solution)/shard_map/all_to_all | solution.py:228
  146.5 0.2 convert_reduce_fusion
  146.7 1.3 pad_maximum_fusion
Async XLA Ops:
  13.3 36.9 %all-to-all-start.2 = ((bf16[16,528,128]{2,1,0:T(8,128)(2,1)}), bf16[16,528,128]{2,1,0:T(8,128)(2,1)S(1)}, u32[]{:S(2)}, u32[]{:S(2)}) async-start(bf16[16,528,128]{2,1,0:T(8,128)(2,1)} %get-tuple-element.4), calls=%async_computation.2 | async-start | bytes 4325376 | tf_op jit(solution)/shard_map/all_to_all | solution.py:225
  50.2 1.3 copy-start.1
  51.6 34.3 %all-to-all-start = ((bf16[16,528,128]{2,1,0:T(8,128)(2,1)}), bf16[16,528,128]{2,1,0:T(8,128)(2,1)S(1)}, u32[]{:S(2)}, u32[]{:S(2)}) async-start(bf16[16,528,128]{2,1,0:T(8,128)(2,1)} %send.2), calls=%async_computation | async-start | bytes 4325376 | tf_op jit(solution)/shard_map/all_to_all | solution.py:225
  85.9 4.6 %copy-start = (bf16[16,528,128]{2,1,0:T(8,128)(2,1)}, bf16[16,528,128]{2,1,0:T(8,128)(2,1)S(1)}, u32[]{:S(2)}) copy-start(bf16[16,528,128]{2,1,0:T(8,128)(2,1)S(1)} %all-to-all-done.data_ref) | copy-start | bytes 6488068
  85.9 30.8 %all-to-all-start.3 = ((bf16[32,128,128]{2,1,0:T(8,128)(2,1)}), bf16[32,128,128]{2,1,0:T(8,128)(2,1)S(1)}, u32[]{:S(2)}, u32[]{:S(2)}) async-start(bf16[32,128,128]{2,1,0:T(8,128)(2,1)} %tally.3), calls=%async_computation.3 | async-start | bytes 2097152 | tf_op jit(solution)/shard_map/all_to_all | solution.py:228
  116.7 29.8 %all-to-all-start.1 = ((bf16[32,128,128]{2,1,0:T(8,128)(2,1)}), bf16[32,128,128]{2,1,0:T(8,128)(2,1)S(1)}, u32[]{:S(2)}, u32[]{:S(2)}) async-start(bf16[32,128,128]{2,1,0:T(8,128)(2,1)} %tally.2), calls=%async_computation.1 | async-start | bytes 2097152 | tf_op jit(solution)/shard_map/all_to_all | solution.py:228

commit v3 on v2

--- a/solution.py
+++ b/solution.py
@@ -116,9 +116,13 @@
     lax.fori_loop(0, count, per_field, 0, unroll=2)
 
 
-def tally_kernel(window, samples, data_ref, out_ref, tags, tiles, tile_at, done):
+def tally_kernel(window, samples, near, first_ref, data_ref, *rest):
+    if near:
+        near_ref, out_ref, tags, tiles, tile_at, done = rest
+    else:
+        out_ref, tags, tiles, tile_at, done = rest
     blocks = data_ref.shape[0]
-    owners = out_ref.shape[0]
+    owners = out_ref.shape[0] + near
     half, pitch = owners // HALVES, LANES // HALVES
     lane = iota((half, LANES), 1)
     tags[...] = jnp.zeros_like(tags)
@@ -145,18 +149,26 @@
     copy.wait()
     row_at = (iota((RQ, blocks * window), 0) + 1).astype(jnp.float32)
 
-    def per_owner(owner, carry):
+    def rows_of(owner):
         part, row = owner // half, owner % half
         picked = []
         for block in range(blocks):
             tile = tile_at[row, part * blocks + block]
             picked.append(data_ref[block, pl.ds(pl.multiple_of(tile * PACK, PACK), window), :])
         matches = one_hot(row_at == tags[pl.ds(owner, 1), : blocks * window])
-        summed = jnp.dot(matches, jnp.concatenate(picked, axis=0), preferred_element_type=jnp.float32)
-        out_ref[owner] = summed.astype(jnp.bfloat16)
-        return carry
-
-    lax.fori_loop(0, owners, per_owner, 0, unroll=4)
+        return jnp.dot(matches, jnp.concatenate(picked, axis=0), preferred_element_type=jnp.float32)
+
+    def per_near(at, carry):
+        near_ref[at] = rows_of((first_ref[0] + at) % owners)
+        return carry
+
+    def per_far(at, carry):
+        out_ref[at] = rows_of((first_ref[0] + near + at) % owners).astype(jnp.bfloat16)
+        return carry
+
+    if near:
+        lax.fori_loop(0, near, per_near, 0, unroll=4)
+    lax.fori_loop(0, owners - near, per_far, 0, unroll=4)
 
 
 def local(outer, inner, sample_ids, features, pair_grad):
@@ -169,7 +181,7 @@
     every = ("tab", "rep")
     groups = [list(range(start, start + inner)) for start in range(0, owners, inner)]
     vmem = pl.BlockSpec(memory_space=pltpu.VMEM)
-    params = pltpu.CompilerParams(vmem_limit_bytes=60 * 2**20)
+    params = pltpu.CompilerParams(vmem_limit_bytes=40 * 2**20)
     ids = sample_ids.T
     by_vector = features.transpose(1, 0, 2)
 
@@ -196,12 +208,15 @@
             name="send",
         )(ids, pair_grad, by_vector)
 
-    def tally(arrived):
+    def tally(arrived, first, near):
+        shapes = [jax.ShapeDtypeStruct((owners - near, RQ, depth), jnp.bfloat16)]
+        if near:
+            shapes = [jax.ShapeDtypeStruct((near, RQ, depth), jnp.float32)] + shapes
         return pl.pallas_call(
-            functools.partial(tally_kernel, window, samples),
-            out_shape=jax.ShapeDtypeStruct((owners, RQ, depth), jnp.bfloat16),
-            in_specs=[vmem],
-            out_specs=vmem,
+            functools.partial(tally_kernel, window, samples, near),
+            out_shape=shapes,
+            in_specs=[pl.BlockSpec(memory_space=pltpu.SMEM), vmem],
+            out_specs=[vmem] * len(shapes),
             scratch_shapes=[
                 pltpu.VMEM((owners, -(-inner * window // LANES) * LANES), jnp.float32),
                 pltpu.VMEM((extra, LANES), jnp.int32),
@@ -211,24 +226,32 @@
             cost_estimate=pl.CostEstimate(
                 flops=2 * owners * inner * window * RQ * depth, bytes_accessed=2 * arrived.size, transcendentals=0
             ),
-            compiler_params=params,
+            compiler_params=pltpu.CompilerParams(vmem_limit_bytes=24 * 2**20),
             name="tally",
-        )(arrived)
-
-    firsts = list(range(0, fields, inner))
-    outgoing = []
-    for first in firsts:
-        outgoing.append(send(first, min(inner, fields - first), first == firsts[-1]))
-    dense_grad = outgoing[-1][0]
-    tables = []
-    for first, sent in zip(firsts, outgoing):
-        arrived = lax.all_to_all(
-            sent[-1], every, split_axis=0, concat_axis=0, tiled=True, axis_index_groups=groups
-        )
-        rows = lax.all_to_all(tally(arrived), every, split_axis=0, concat_axis=0, tiled=True)
-        rows = rows.reshape(outer, inner, RQ, depth)[:, : min(inner, fields - first)]
-        tables.append(rows.astype(jnp.float32).sum(axis=0))
-    return jnp.concatenate(tables, axis=0), dense_grad
+        )(jnp.reshape(first, (1,)).astype(jnp.int32), arrived)
+
+    def exchange(blocks, groups):
+        return lax.all_to_all(blocks, every, split_axis=0, concat_axis=0, tiled=True, axis_index_groups=groups)
+
+    def relayed(sent):
+        mine, others = tally(exchange(sent, groups), lax.axis_index(every) // inner * inner, inner)
+        others = others.reshape(outer - 1, inner, RQ, depth)
+        total = mine
+        for hop in range(1, outer):
+            total += lax.ppermute(
+                others[hop - 1], every, [(at, (at + hop * inner) % owners) for at in range(owners)]
+            ).astype(jnp.float32)
+        return exchange(total.astype(jnp.bfloat16), groups).astype(jnp.float32)
+
+    def direct(sent):
+        (rows,) = tally(exchange(sent, groups), jnp.int32(0), 0)
+        return exchange(rows, None).reshape(outer, inner, RQ, depth).astype(jnp.float32).sum(axis=0)
+
+    tail = fields - fields % inner
+    dense_grad, sent = send(tail, fields - tail, True)
+    last = relayed(sent)[: fields - tail]
+    tables = [direct(send(first, inner, False)[0]) for first in range(0, tail, inner)]
+    return jnp.concatenate(tables + [last], axis=0), dense_grad
 
 
 def solution(mesh):

time: 149 us -> 145 us (0.973)
  Pallas kernels: 42.2 us -> 33.1 us
  local copies, waits for them, and re-layouts: 1.34 us -> 8.36 us
  waiting for transfers between devices: 84 us -> 77.4 us
  starting transfers between devices: 18.3 us -> 21.8 us
    all_to_all x4, waiting for transfers between devices: 84 us -> 47.7 us  [exchange(): lax.all_to_all(blocks, every, split_axis=0, concat_axis=0, tiled=True, ax...]
    ppermute x0 -> x1, waiting for transfers between devices: none -> 29.8 us  [relayed(): lax.ppermute(others[hop - 1], every, [(at, (at + hop * inner) % owners) f...]
    unnamed x4 -> x16, local copies, waits for them, and re-layouts: 1.34 us -> 8.36 us
    pallas_call x2, Pallas kernels: 28.6 us -> 21.8 us  [send(): pl.pallas_call(functools.partial(send_kernel, first, count, dense, owners...]
    ppermute x0 -> x1, starting transfers between devices: none -> 2.66 us  [relayed(): lax.ppermute(others[hop - 1], every, [(at, (at + hop * inner) % owners) f...]
    pallas_call x2, Pallas kernels: 13.6 us -> 11.3 us  [tally(): pl.pallas_call(functools.partial(tally_kernel, window, samples, near), ou...]
  transfers between devices with their start and end apart: 4 -> 5, of which waited for: 4 -> 5; matrix products, arithmetic and copies ran while one was open for 0% -> 1% of each run, Pallas kernels for 9% -> 8%
where the time goes in v3:
time: 145 us; the launch traced here: 144 us
  waiting for transfers between devices  77.4 us (53%)
  Pallas kernels  33.1 us (23%)
  starting transfers between devices  21.8 us (15%)
  local copies, waits for them, and re-layouts  8.36 us (6%)
  other arithmetic  2.47 us (2%)
    all_to_all x4, waiting for transfers between devices, exchange(): lax.all_to_all(blocks, every, split_axis=0, concat_axis=0, tiled=True, ax...  47.7 us
    ppermute x1, waiting for transfers between devices, relayed(): lax.ppermute(others[hop - 1], every, [(at, (at + hop * inner) % owners) f...  29.8 us
    pallas_call x2, Pallas kernels, send(): pl.pallas_call(functools.partial(send_kernel, first, count, dense, owners...  21.8 us
    all_to_all x4, starting transfers between devices, exchange(): lax.all_to_all(blocks, every, split_axis=0, concat_axis=0, tiled=True, ax...  19.1 us
    pallas_call x2, Pallas kernels, tally(): pl.pallas_call(functools.partial(tally_kernel, window, samples, near), ou...  11.3 us
    unnamed x16, local copies, waits for them, and re-layouts  8.36 us
  transfers between devices with their start and end apart: 5, of which 5 were waited for; matrix products, arithmetic and copies ran while one was open for 1% of the time, Pallas kernels for 8%

profile of v3, /device:TPU:0, one launch (start us, length us, event | category | flops | bytes accessed | tf_op | source)
XLA Modules:
  0.0 143.9 jit_solution(3531674645757114842)
XLA Ops:
  0.6 2.0 %copy-done = bf16[512,27,128]{2,0,1:T(8,128)(2,1)S(1)} copy-done((bf16[512,27,128]{2,0,1:T(8,128)(2,1)S(1)}, bf16[512,27,128]{2,0,1:T(8,128)(2,1)}, u32[]{:S(2)}) %copy-start) | copy-done | bytes 3538968
  2.6 1.0 copy-done.4
  3.6 0.8 copy-done.6
  4.5 9.4 %send.3 = (f32[512,128]{1,0:T(8,128)}, bf16[16,528,128]{2,1,0:T(8,128)(2,1)S(1)}) custom-call(s32[26,512]{1,0:T(8,128)S(1)} %bitcast.7, bf16[351,512]{1,0:T(8,128)(2,1)S(1)} %copy-done.4, bf16[27,512,128]{2,1,0:T(8,128)(2,1)S(1)} %bitcast.5), custom_call_target="tpu_custom_call" | custom-call | flops 738197504 | bytes 3538944 | tf_op jit(solution)/shard_map/send/pallas_call | solution.py:193
  13.9 1.4 copy-done.3
  15.3 6.6 %all-to-all-start.2 = ((bf16[16,528,128]{2,1,0:T(8,128)(2,1)}), bf16[16,528,128]{2,1,0:T(8,128)(2,1)}, u32[]{:S(2)}, u32[]{:S(2)}) async-start(bf16[16,528,128]{2,1,0:T(8,128)(2,1)} %copy-done.3), calls=%async_computation.2 | async-start | bytes 4325376 | tf_op jit(solution)/shard_map/all_to_all | solution.py:234
  21.9 1.0 copy-done.5
  22.9 0.8 copy-done.7
  23.8 12.3 %send.2 = bf16[16,528,128]{2,1,0:T(8,128)(2,1)S(1)} custom-call(s32[26,512]{1,0:T(8,128)S(1)} %bitcast.8, bf16[351,512]{1,0:T(8,128)(2,1)S(1)} %copy-done.5, bf16[27,512,128]{2,1,0:T(8,128)(2,1)S(1)} %bitcast.6), custom_call_target="tpu_custom_call" | custom-call | flops 1073741824 | bytes 3538944 | tf_op jit(solution)/shard_map/send/pallas_call | solution.py:193
  36.1 1.3 copy-done.2
  37.5 15.1 %all-to-all-done.2.data_ref = bf16[16,528,128]{2,1,0:T(8,128)(2,1)} async-done(((bf16[16,528,128]{2,1,0:T(8,128)(2,1)}), bf16[16,528,128]{2,1,0:T(8,128)(2,1)}, u32[]{:S(2)}, u32[]{:S(2)}) %all-to-all-start.2) | async-done | bytes 2162720 | tf_op jit(solution)/shard_map/all_to_all | solution.py:234
  52.6 3.7 %all-to-all-start = ((bf16[16,528,128]{2,1,0:T(8,128)(2,1)}), bf16[16,528,128]{2,1,0:T(8,128)(2,1)S(1)}, u32[]{:S(2)}, u32[]{:S(2)}) async-start(bf16[16,528,128]{2,1,0:T(8,128)(2,1)} %copy-done.2), calls=%async_computation | async-start | bytes 4325376 | tf_op jit(solution)/shard_map/all_to_all | solution.py:234
  56.3 6.0 %tally.3 = (f32[16,128,128]{2,1,0:T(8,128)S(1)}, bf16[16,128,128]{2,1,0:T(8,128)(2,1)S(1)}) custom-call(s32[1]{0:T(128)} %bitcast.3.first_ref, bf16[16,528,128]{2,1,0:T(8,128)(2,1)} %all-to-all-done.2.data_ref), custom_call_target="tpu_custom_call" | custom-call | flops 805306368 | bytes 2162688 | tf_op jit(solution)/shard_map/tally/pallas_call | solution.py:215
  62.3 2.7 %collective-permute-start = (bf16[16,128,128]{2,1,0:T(8,128)(2,1)S(1)}, bf16[16,128,128]{2,1,0:T(8,128)(2,1)S(1)}, u32[]{:S(2)}, u32[]{:S(2)}) collective-permute-start(bf16[16,128,128]{2,1,0:T(8,128)(2,1)S(1)} %get-tuple-element.8), channel_id=1, source_target_pairs={{0,16},{1,17},{2,18},{3,19},{4,20},{5,21},{6,22},{7,23},{8,24},{9,... | collective-permute-start | bytes 1572872 | tf_op jit(solution)/shard_map/ppermute | solution.py:241
  65.0 29.8 %collective-permute-done = bf16[16,128,128]{2,1,0:T(8,128)(2,1)S(1)} collective-permute-done((bf16[16,128,128]{2,1,0:T(8,128)(2,1)S(1)}, bf16[16,128,128]{2,1,0:T(8,128)(2,1)S(1)}, u32[]{:S(2)}, u32[]{:S(2)}) %collective-permute-start) | collective-permute-done | bytes 524320 | tf_op jit(solution)/shard_map/ppermute | solution.py:241
  94.8 0.9 add_convert_fusion
  95.7 1.2 all-to-all-done.data_ref
  96.9 6.1 %all-to-all-start.3 = ((bf16[16,128,128]{2,1,0:T(8,128)(2,1)}), bf16[16,128,128]{2,1,0:T(8,128)(2,1)S(1)}, u32[]{:S(2)}, u32[]{:S(2)}) async-start(bf16[16,128,128]{2,1,0:T(8,128)(2,1)} %add_convert_fusion), calls=%async_computation.3 | async-start | bytes 1048576 | tf_op jit(solution)/shard_map/all_to_all | solution.py:234
  103.0 5.3 %tally.2 = bf16[32,128,128]{2,1,0:T(8,128)(2,1)} custom-call(s32[1]{0:T(128)} %constant.20.clone.1.first_ref, bf16[16,528,128]{2,1,0:T(8,128)(2,1)S(1)} %all-to-all-done.data_ref), custom_call_target="tpu_custom_call" | custom-call | flops 805306368 | bytes 2162688 | tf_op jit(solution)/shard_map/tally/pallas_call | solution.py:215
  108.4 5.2 %all-to-all-done.3 = bf16[16,128,128]{2,1,0:T(8,128)(2,1)S(1)} async-done(((bf16[16,128,128]{2,1,0:T(8,128)(2,1)}), bf16[16,128,128]{2,1,0:T(8,128)(2,1)S(1)}, u32[]{:S(2)}, u32[]{:S(2)}) %all-to-all-start.3) | async-done | bytes 524320 | tf_op jit(solution)/shard_map/all_to_all | solution.py:234
  113.6 2.6 %all-to-all-start.1 = ((bf16[32,128,128]{2,1,0:T(8,128)(2,1)}), bf16[32,128,128]{2,1,0:T(8,128)(2,1)S(1)}, u32[]{:S(2)}, u32[]{:S(2)}) async-start(bf16[32,128,128]{2,1,0:T(8,128)(2,1)} %tally.2), calls=%async_computation.1 | async-start | bytes 2097152 | tf_op jit(solution)/shard_map/all_to_all | solution.py:234
  116.3 26.1 %all-to-all-done.1 = bf16[32,128,128]{2,1,0:T(8,128)(2,1)S(1)} async-done(((bf16[32,128,128]{2,1,0:T(8,128)(2,1)}), bf16[32,128,128]{2,1,0:T(8,128)(2,1)S(1)}, u32[]{:S(2)}, u32[]{:S(2)}) %all-to-all-start.1) | async-done | bytes 1048608 | tf_op jit(solution)/shard_map/all_to_all | solution.py:234
  142.4 0.2 convert_reduce_fusion
  142.6 1.3 pad_maximum_fusion
  (10 shorter events, 0.1 us)
Async XLA Ops:
  0.6 2.0 %copy-start = (bf16[512,27,128]{2,0,1:T(8,128)(2,1)S(1)}, bf16[512,27,128]{2,0,1:T(8,128)(2,1)}, u32[]{:S(2)}) copy-start(bf16[512,27,128]{2,0,1:T(8,128)(2,1)} %param.4) | copy-start | bytes 10616836
  2.6 1.0 copy-start.4
  3.6 0.8 copy-start.6
  13.9 1.4 copy-start.3
  15.3 6.6 %copy-start.1 = (bf16[512,27,128]{2,0,1:T(8,128)(2,1)S(1)}, bf16[512,27,128]{2,0,1:T(8,128)(2,1)}, u32[]{:S(2)}) copy-start(bf16[512,27,128]{2,0,1:T(8,128)(2,1)} %param.4) | copy-start | bytes 10616836
  15.3 37.3 %all-to-all-start.2 = ((bf16[16,528,128]{2,1,0:T(8,128)(2,1)}), bf16[16,528,128]{2,1,0:T(8,128)(2,1)}, u32[]{:S(2)}, u32[]{:S(2)}) async-start(bf16[16,528,128]{2,1,0:T(8,128)(2,1)} %copy-done.3), calls=%async_computation.2 | async-start | bytes 4325376 | tf_op jit(solution)/shard_map/all_to_all | solution.py:234
  21.9 1.0 copy-start.5
  22.9 0.8 copy-start.7
  36.1 1.4 copy-start.2
  52.6 44.3 %all-to-all-start = ((bf16[16,528,128]{2,1,0:T(8,128)(2,1)}), bf16[16,528,128]{2,1,0:T(8,128)(2,1)S(1)}, u32[]{:S(2)}, u32[]{:S(2)}) async-start(bf16[16,528,128]{2,1,0:T(8,128)(2,1)} %copy-done.2), calls=%async_computation | async-start | bytes 4325376 | tf_op jit(solution)/shard_map/all_to_all | solution.py:234
  62.3 32.4 %collective-permute-start = (bf16[16,128,128]{2,1,0:T(8,128)(2,1)S(1)}, bf16[16,128,128]{2,1,0:T(8,128)(2,1)S(1)}, u32[]{:S(2)}, u32[]{:S(2)}) collective-permute-start(bf16[16,128,128]{2,1,0:T(8,128)(2,1)S(1)} %get-tuple-element.8), channel_id=1, source_target_pairs={{0,16},{1,17},{2,18},{3,19},{4,20},{5,21},{6,22},{7,23},{8,24},{9,... | collective-permute-start | bytes 1572872 | tf_op jit(solution)/shard_map/ppermute | solution.py:241
  96.9 16.6 %all-to-all-start.3 = ((bf16[16,128,128]{2,1,0:T(8,128)(2,1)}), bf16[16,128,128]{2,1,0:T(8,128)(2,1)S(1)}, u32[]{:S(2)}, u32[]{:S(2)}) async-start(bf16[16,128,128]{2,1,0:T(8,128)(2,1)} %add_convert_fusion), calls=%async_computation.3 | async-start | bytes 1048576 | tf_op jit(solution)/shard_map/all_to_all | solution.py:234
  113.6 28.8 %all-to-all-start.1 = ((bf16[32,128,128]{2,1,0:T(8,128)(2,1)}), bf16[32,128,128]{2,1,0:T(8,128)(2,1)S(1)}, u32[]{:S(2)}, u32[]{:S(2)}) async-start(bf16[32,128,128]{2,1,0:T(8,128)(2,1)} %tally.2), calls=%async_computation.1 | async-start | bytes 2097152 | tf_op jit(solution)/shard_map/all_to_all | solution.py:234

commit v4 on v2

--- a/solution.py
+++ b/solution.py
@@ -13,6 +13,8 @@
 PACK = 16
 SUB = 8
 HALVES = 2
+PARTS = 4
+GROUP = LANES // PARTS
 
 
 def iota(shape, dim):
@@ -23,7 +25,7 @@
     return jnp.where(hit, 1.0, 0.0).astype(jnp.bfloat16)
 
 
-def order_fields(first, count, owners, window, ids_ref, payload_ref, rank_ref, mine):
+def order_fields(first, count, owners, window, ids_ref, store, rank_ref, mine):
     samples = ids_ref.shape[1]
     pitch = LANES // HALVES
     last_tile = (samples - window) // PACK
@@ -56,20 +58,59 @@
         half = owners // HALVES
         row = tags[:half] + pltpu.roll(tags[half:], pitch, 1)
         row = jnp.where(lane == pitch - 1, tile[:half], jnp.where(lane == LANES - 1, tile[half:], row))
-        payload_ref[at, samples:, :] = row.astype(jnp.bfloat16)
-
-
-def send_kernel(first, count, dense, owners, window, ids_ref, pairs_ref, feat_ref, *rest):
-    if dense:
+        store(at, row.astype(jnp.bfloat16))
+
+
+def fold(block):
+    kept = block.shape[0] * (PARTS - 1) // PARTS
+    moved = [pltpu.roll(block[kept:], (PARTS - 1 - part) * GROUP, 1) for part in range(PARTS - 1)]
+    last_group = iota((kept, LANES), 1) >= LANES - GROUP
+    return jnp.where(last_group, jnp.concatenate(moved, axis=0), block[:kept])
+
+
+def unfold(block):
+    rows = block.shape[0] // (PARTS - 1)
+    group = iota((rows, LANES), 1) // GROUP
+    parts = [pltpu.roll(block[part * rows : (part + 1) * rows], (part + 1) * GROUP, 1) for part in range(PARTS - 1)]
+    return jnp.where(group == 0, parts[0], jnp.where(group == 1, parts[1], parts[2]))
+
+
+def fold_last(blocks):
+    rows = blocks[0].shape[0] // PARTS
+    kept = rows * (PARTS - 1)
+    group = iota((kept, LANES), 1) // GROUP
+    out = jnp.zeros((kept, LANES), blocks[0].dtype)
+    tails = [jnp.zeros((rows, LANES), blocks[0].dtype)] * (PARTS - 1)
+    for part, block in enumerate(blocks):
+        out = jnp.where(group == part, pltpu.roll(block[:kept], (part + 1) * GROUP, 1), out)
+        tails[part] = block[kept:]
+    return jnp.where(group == PARTS - 1, jnp.concatenate(tails, axis=0), out)
+
+
+def send_kernel(first, count, tail, owners, window, ids_ref, pairs_ref, feat_ref, *rest):
+    if tail:
         dense_ref, payload_ref, rank_ref, mine, weights, grads = rest
     else:
         payload_ref, rank_ref, mine, weights, grads = rest
+    dense = tail
     vectors, samples, depth = feat_ref.shape
     span = 2 * LANES
-    order_fields(first, count, owners, window, ids_ref, payload_ref, rank_ref, mine)
+    body = samples * (PARTS - 1) // PARTS if tail else samples
+    extra = owners // HALVES
+    whole = count + -(-count // 2) if tail else count
     for at in range(count, payload_ref.shape[0]):
-        payload_ref[at] = jnp.zeros(payload_ref.shape[1:], jnp.bfloat16)
-
+        payload_ref[at, body:] = jnp.zeros((payload_ref.shape[1] - body, LANES), jnp.bfloat16)
+    for at in range(whole, payload_ref.shape[0]):
+        payload_ref[at, :body] = jnp.zeros((body, LANES), jnp.bfloat16)
+
+    def store(at, row):
+        payload_ref[at, body : body + extra, :] = row
+        if tail:
+            payload_ref[at, body + extra :, :] = row
+            place = body + at % 2 * extra
+            payload_ref[count + at // 2, place : place + extra, :] = row
+
+    order_fields(first, count, owners, window, ids_ref, store, rank_ref, mine)
     targets = ([0] if dense else []) + list(range(first + 1, first + 1 + count))
     pairs = pairs_ref[...].astype(jnp.float32).T.astype(jnp.bfloat16)
     pair_at = iota((pairs.shape[1], span), 0)
@@ -107,24 +148,32 @@
     lax.fori_loop(0, samples // PACK, per_group, 0, unroll=2)
     slot_at = iota((samples, samples), 0).astype(jnp.float32)
 
-    def per_field(at, carry):
+    def placed(at):
         placing = one_hot(slot_at == rank_ref[pl.ds(at, 1), :])
-        placed = jnp.dot(placing, grads[at], preferred_element_type=jnp.float32)
-        payload_ref[at, :samples, :] = placed.astype(jnp.bfloat16)
-        return carry
-
-    lax.fori_loop(0, count, per_field, 0, unroll=2)
-
-
-def tally_kernel(window, samples, data_ref, out_ref, tags, tiles, tile_at, done):
-    blocks = data_ref.shape[0]
-    owners = out_ref.shape[0]
-    half, pitch = owners // HALVES, LANES // HALVES
+        return jnp.dot(placing, grads[at], preferred_element_type=jnp.float32)
+
+    if tail:
+        for at in range(0, count, 2):
+            blocks = [placed(each) for each in range(at, min(at + 2, count))]
+            for each, block in enumerate(blocks):
+                payload_ref[at + each, :body, :] = fold(block).astype(jnp.bfloat16)
+            payload_ref[count + at // 2, :body, :] = fold_last(blocks).astype(jnp.bfloat16)
+    else:
+
+        def per_field(at, carry):
+            payload_ref[at, :body, :] = placed(at).astype(jnp.bfloat16)
+            return carry
+
+        lax.fori_loop(0, count, per_field, 0, unroll=2)
+
+
+def read_tags(window, blocks, first_row, data_ref, tags, tiles):
+    half, pitch = tiles.shape[0], LANES // HALVES
     lane = iota((half, LANES), 1)
     tags[...] = jnp.zeros_like(tags)
     found = jnp.zeros((half, LANES), jnp.float32)
     for block in range(blocks):
-        rows = data_ref[block, samples:, :].astype(jnp.float32)
+        rows = data_ref[block, first_row : first_row + half, :].astype(jnp.float32)
         column, offset = divmod(block * window, LANES)
         for part in range(HALVES):
             own = slice(part * half, (part + 1) * half)
@@ -140,23 +189,76 @@
                 after = slice((column + 1) * LANES, (column + 2) * LANES)
                 tags[own, after] = jnp.where(lane < window - fits, shifted, tags[own, after])
     tiles[...] = found.astype(jnp.int32)
+
+
+def rows_of(window, owner, sorted_ref, tags, tile_at):
+    blocks = sorted_ref.shape[0]
+    half = tile_at.shape[0]
+    part, row = owner // half, owner % half
+    row_at = (iota((RQ, blocks * window), 0) + 1).astype(jnp.float32)
+    picked = []
+    for block in range(blocks):
+        tile = tile_at[row, part * blocks + block]
+        picked.append(sorted_ref[block, pl.ds(pl.multiple_of(tile * PACK, PACK), window), :])
+    matches = one_hot(row_at == tags[pl.ds(owner, 1), : blocks * window])
+    return jnp.dot(matches, jnp.concatenate(picked, axis=0), preferred_element_type=jnp.float32)
+
+
+def tally_kernel(window, samples, data_ref, tail_ref, out_ref, tags, tiles, tile_at, done):
+    read_tags(window, data_ref.shape[0], samples, data_ref, tags, tiles)
     copy = pltpu.make_async_copy(tiles, tile_at, done)
     copy.start()
+    out_ref[:, RQ:, :] = tail_ref[...]
     copy.wait()
-    row_at = (iota((RQ, blocks * window), 0) + 1).astype(jnp.float32)
 
     def per_owner(owner, carry):
-        part, row = owner // half, owner % half
-        picked = []
-        for block in range(blocks):
-            tile = tile_at[row, part * blocks + block]
-            picked.append(data_ref[block, pl.ds(pl.multiple_of(tile * PACK, PACK), window), :])
-        matches = one_hot(row_at == tags[pl.ds(owner, 1), : blocks * window])
-        summed = jnp.dot(matches, jnp.concatenate(picked, axis=0), preferred_element_type=jnp.float32)
-        out_ref[owner] = summed.astype(jnp.bfloat16)
+        out_ref[owner, :RQ, :] = rows_of(window, owner, data_ref, tags, tile_at).astype(jnp.bfloat16)
         return carry
 
-    lax.fori_loop(0, owners, per_owner, 0, unroll=4)
+    lax.fori_loop(0, out_ref.shape[0], per_owner, 0, unroll=4)
+
+
+def tally_tail_kernel(window, samples, data_ref, out_ref, unfolded, tags, tags_b, tiles, tiles_b, tile_at, tile_at_b, done):
+    blocks = data_ref.shape[0]
+    body = samples * (PARTS - 1) // PARTS
+    read_tags(window, blocks, body, data_ref, tags, tiles)
+    read_tags(window, blocks, body + tiles.shape[0], data_ref, tags_b, tiles_b)
+    copy = pltpu.make_async_copy(tiles, tile_at, done.at[0])
+    copy_b = pltpu.make_async_copy(tiles_b, tile_at_b, done.at[1])
+    copy.start()
+    copy_b.start()
+    for block in range(blocks):
+        unfolded[block, :body, :] = data_ref[block, :body, :]
+        unfolded[block, body:, :] = unfold(data_ref[block, :body, :].astype(jnp.float32)).astype(jnp.bfloat16)
+    copy.wait()
+    copy_b.wait()
+    second = iota((RQ, LANES), 1) // GROUP == 1
+
+    def per_owner(owner, carry):
+        rows = rows_of(window, owner, unfolded, tags, tile_at)
+        rows_b = rows_of(window, owner, unfolded, tags_b, tile_at_b)
+        out_ref[owner] = fold(jnp.where(second, rows_b, rows)).astype(jnp.bfloat16)
+        return carry
+
+    lax.fori_loop(0, out_ref.shape[0], per_owner, 0, unroll=2)
+
+
+def finish_kernel(count, data_ref, table_ref):
+    inner = data_ref.shape[1]
+    kept = RQ * (PARTS - 1) // PARTS
+    rest = RQ - kept
+    tails = []
+    for at in range(inner):
+        total = jnp.sum(data_ref[:, at].astype(jnp.float32), axis=0)
+        table_ref[at] = total[:RQ]
+        tails.append(total[RQ:])
+    own = iota((RQ, LANES), 1) < LANES - GROUP
+    for at in range(count):
+        part, block, other = at % 2, tails[at], tails[count + at // 2]
+        main = jnp.concatenate([block, unfold(block)], axis=0)
+        last = pltpu.roll(other, (PARTS - 1 - part) * GROUP, 1)
+        last = jnp.concatenate([last, other[part * rest : (part + 1) * rest]], axis=0)
+        table_ref[inner + at] = jnp.where(own, main, last)
 
 
 def local(outer, inner, sample_ids, features, pair_grad):
@@ -166,20 +268,27 @@
     capacity = 2 * samples // owners
     window = min(-(-(PACK - 1 + capacity) // PACK) * PACK, samples)
     extra = owners // HALVES
+    tail = fields - inner
+    if depth != LANES or not 0 < tail + -(-tail // 2) <= inner:
+        raise ValueError("unsupported sizes")
     every = ("tab", "rep")
     groups = [list(range(start, start + inner)) for start in range(0, owners, inner)]
     vmem = pl.BlockSpec(memory_space=pltpu.VMEM)
-    params = pltpu.CompilerParams(vmem_limit_bytes=60 * 2**20)
+    params = pltpu.CompilerParams(vmem_limit_bytes=40 * 2**20)
     ids = sample_ids.T
     by_vector = features.transpose(1, 0, 2)
-
-    def send(first, count, dense):
-        targets = count + dense
-        shapes = [jax.ShapeDtypeStruct((inner, samples + extra, depth), jnp.bfloat16)]
-        if dense:
+    tail_samples = samples * (PARTS - 1) // PARTS
+    tail_rows = RQ * (PARTS - 1) // PARTS
+    tag_shape = (owners, -(-inner * window // LANES) * LANES)
+
+    def send(first, count, is_tail):
+        targets = count + is_tail
+        rows = tail_samples + 2 * extra if is_tail else samples + extra
+        shapes = [jax.ShapeDtypeStruct((inner, rows, depth), jnp.bfloat16)]
+        if is_tail:
             shapes = [jax.ShapeDtypeStruct((samples, depth), jnp.float32)] + shapes
         return pl.pallas_call(
-            functools.partial(send_kernel, first, count, dense, owners, window),
+            functools.partial(send_kernel, first, count, is_tail, owners, window),
             out_shape=shapes,
             in_specs=[vmem] * 3,
             out_specs=[vmem] * len(shapes),
@@ -196,39 +305,59 @@
             name="send",
         )(ids, pair_grad, by_vector)
 
-    def tally(arrived):
-        return pl.pallas_call(
-            functools.partial(tally_kernel, window, samples),
-            out_shape=jax.ShapeDtypeStruct((owners, RQ, depth), jnp.bfloat16),
-            in_specs=[vmem],
-            out_specs=vmem,
-            scratch_shapes=[
-                pltpu.VMEM((owners, -(-inner * window // LANES) * LANES), jnp.float32),
-                pltpu.VMEM((extra, LANES), jnp.int32),
-                pltpu.SMEM((extra, LANES), jnp.int32),
-                pltpu.SemaphoreType.DMA,
-            ],
-            cost_estimate=pl.CostEstimate(
-                flops=2 * owners * inner * window * RQ * depth, bytes_accessed=2 * arrived.size, transcendentals=0
-            ),
-            compiler_params=params,
-            name="tally",
-        )(arrived)
-
-    firsts = list(range(0, fields, inner))
-    outgoing = []
-    for first in firsts:
-        outgoing.append(send(first, min(inner, fields - first), first == firsts[-1]))
-    dense_grad = outgoing[-1][0]
-    tables = []
-    for first, sent in zip(firsts, outgoing):
-        arrived = lax.all_to_all(
-            sent[-1], every, split_axis=0, concat_axis=0, tiled=True, axis_index_groups=groups
-        )
-        rows = lax.all_to_all(tally(arrived), every, split_axis=0, concat_axis=0, tiled=True)
-        rows = rows.reshape(outer, inner, RQ, depth)[:, : min(inner, fields - first)]
-        tables.append(rows.astype(jnp.float32).sum(axis=0))
-    return jnp.concatenate(tables, axis=0), dense_grad
+    def exchange(blocks, groups):
+        return lax.all_to_all(blocks, every, split_axis=0, concat_axis=0, tiled=True, axis_index_groups=groups)
+
+    small = pltpu.CompilerParams(vmem_limit_bytes=28 * 2**20)
+    cost = pl.CostEstimate(
+        flops=2 * owners * inner * window * RQ * depth, bytes_accessed=4 * inner * samples * depth, transcendentals=0
+    )
+    dense_grad, sent_tail = send(inner, tail, True)
+    arrived_tail = exchange(sent_tail, groups)
+    rows_tail = pl.pallas_call(
+        functools.partial(tally_tail_kernel, window, samples),
+        out_shape=jax.ShapeDtypeStruct((owners, tail_rows, depth), jnp.bfloat16),
+        in_specs=[vmem],
+        out_specs=vmem,
+        scratch_shapes=[
+            pltpu.VMEM((inner, samples, depth), jnp.bfloat16),
+            pltpu.VMEM(tag_shape, jnp.float32),
+            pltpu.VMEM(tag_shape, jnp.float32),
+            pltpu.VMEM((extra, LANES), jnp.int32),
+            pltpu.VMEM((extra, LANES), jnp.int32),
+            pltpu.SMEM((extra, LANES), jnp.int32),
+            pltpu.SMEM((extra, LANES), jnp.int32),
+            pltpu.SemaphoreType.DMA((2,)),
+        ],
+        cost_estimate=cost,
+        compiler_params=small,
+        name="tally_tail",
+    )(arrived_tail)
+    arrived = exchange(send(0, inner, False)[0], groups)
+    rows = pl.pallas_call(
+        functools.partial(tally_kernel, window, samples),
+        out_shape=jax.ShapeDtypeStruct((owners, RQ + tail_rows, depth), jnp.bfloat16),
+        in_specs=[vmem] * 2,
+        out_specs=vmem,
+        scratch_shapes=[
+            pltpu.VMEM(tag_shape, jnp.float32),
+            pltpu.VMEM((extra, LANES), jnp.int32),
+            pltpu.SMEM((extra, LANES), jnp.int32),
+            pltpu.SemaphoreType.DMA,
+        ],
+        cost_estimate=cost,
+        compiler_params=small,
+        name="tally",
+    )(arrived, rows_tail)
+    table_grad = pl.pallas_call(
+        functools.partial(finish_kernel, tail),
+        out_shape=jax.ShapeDtypeStruct((fields, RQ, depth), jnp.float32),
+        in_specs=[vmem],
+        out_specs=vmem,
+        compiler_params=small,
+        name="finish",
+    )(exchange(rows, None).reshape(outer, inner, RQ + tail_rows, depth))
+    return table_grad, dense_grad
 
 
 def solution(mesh):

time: 149 us -> 133 us (0.89)
  waiting for transfers between devices: 84 us -> 29.1 us
  blocking collectives: 0 us -> 47.1 us
  starting transfers between devices: 18.3 us -> 10.1 us
  local copies, waits for them, and re-layouts: 1.34 us -> 8.17 us
  Pallas kernels: 42.2 us -> 37.6 us
  other arithmetic: 1.6 us -> 0 us
    all_to_all x4 -> x2, waiting for transfers between devices: 84 us -> 29.1 us  [exchange(): lax.all_to_all(blocks, every, split_axis=0, concat_axis=0, tiled=True, ax...]
    all_to_all x0 -> x1, blocking collectives: none -> 47.1 us  [exchange(): lax.all_to_all(blocks, every, split_axis=0, concat_axis=0, tiled=True, ax...]
    all_to_all x4 -> x2, starting transfers between devices: 18.3 us -> 10.1 us  [exchange(): lax.all_to_all(blocks, every, split_axis=0, concat_axis=0, tiled=True, ax...]
    unnamed x4 -> x16, local copies, waits for them, and re-layouts: 1.34 us -> 8.17 us
    pallas_call x4 -> x5, Pallas kernels: 42.2 us -> 37.6 us  [the longest x2 21.5 us: send(): pl.pallas_call(functools.partial(send_kernel, first, count, is_tail, owne...]
  transfers between devices with their start and end apart: 4 -> 2, of which waited for: 4 -> 2; matrix products, arithmetic and copies ran while one was open for 0% -> 0% of each run, Pallas kernels for 9% -> 8%
where the time goes in v4:
time: 133 us
  blocking collectives  47.1 us (35%)
  Pallas kernels  37.6 us (28%)
  waiting for transfers between devices  29.1 us (22%)
  starting transfers between devices  10.1 us (8%)
  local copies, waits for them, and re-layouts  8.17 us (6%)
    all_to_all x1, blocking collectives, exchange(): lax.all_to_all(blocks, every, split_axis=0, concat_axis=0, tiled=True, ax...  47.1 us
    all_to_all x2, waiting for transfers between devices, exchange(): lax.all_to_all(blocks, every, split_axis=0, concat_axis=0, tiled=True, ax...  29.1 us
    pallas_call x2, Pallas kernels, send(): pl.pallas_call(functools.partial(send_kernel, first, count, is_tail, owne...  21.5 us
    pallas_call x1, Pallas kernels, local(): pl.pallas_call(functools.partial(tally_tail_kernel, window, samples), out...  10.3 us
    all_to_all x2, starting transfers between devices, exchange(): lax.all_to_all(blocks, every, split_axis=0, concat_axis=0, tiled=True, ax...  10.1 us
    unnamed x16, local copies, waits for them, and re-layouts  8.17 us
    pallas_call x1, Pallas kernels, local(): pl.pallas_call(functools.partial(tally_kernel, window, samples), out_shap...  4.18 us
  transfers between devices with their start and end apart: 2, of which 2 were waited for; matrix products, arithmetic and copies ran while one was open for 0% of the time, Pallas kernels for 8%

profile of v4, /device:TPU:0, one launch (start us, length us, event | category | flops | bytes accessed | tf_op | source)
XLA Modules:
  0.0 132.7 jit_solution(17313477579567580328)
XLA Ops:
  0.6 0.0 copy-start
  0.6 2.0 %copy-done = bf16[512,27,128]{2,0,1:T(8,128)(2,1)S(1)} copy-done((bf16[512,27,128]{2,0,1:T(8,128)(2,1)S(1)}, bf16[512,27,128]{2,0,1:T(8,128)(2,1)}, u32[]{:S(2)}) %copy-start) | copy-done | bytes 3538968
  2.6 0.0 copy-start.4
  2.6 1.0 copy-done.4
  3.6 0.0 copy-start.6
  3.6 0.8 copy-done.6
  4.5 0.0 copy-start.1
  4.5 9.2 %send.3 = (f32[512,128]{1,0:T(8,128)}, bf16[16,416,128]{2,1,0:T(8,128)(2,1)S(1)}) custom-call(s32[26,512]{1,0:T(8,128)S(1)} %bitcast.6, bf16[351,512]{1,0:T(8,128)(2,1)S(1)} %copy-done.4, bf16[27,512,128]{2,1,0:T(8,128)(2,1)S(1)} %bitcast.3), custom_call_target="tpu_custom_call" | custom-call | flops 738197504 | bytes 3538944 | tf_op jit(solution)/shard_map/send/pallas_call | solution.py:290
  13.7 1.2 copy-done.3
  14.8 6.4 %all-to-all-start.1 = ((bf16[16,416,128]{2,1,0:T(8,128)(2,1)}), bf16[16,416,128]{2,1,0:T(8,128)(2,1)}, u32[]{:S(2)}, u32[]{:S(2)}) async-start(bf16[16,416,128]{2,1,0:T(8,128)(2,1)} %copy-done.3), calls=%async_computation.1 | async-start | bytes 3407872 | tf_op jit(solution)/shard_map/all_to_all | solution.py:309
  21.2 0.0 copy-done.1
  21.2 0.0 copy-start.5
  21.2 1.0 copy-done.5
  22.2 0.8 copy-done.7
  23.1 12.3 %send.2 = bf16[16,528,128]{2,1,0:T(8,128)(2,1)S(1)} custom-call(s32[26,512]{1,0:T(8,128)S(1)} %bitcast.7, bf16[351,512]{1,0:T(8,128)(2,1)S(1)} %copy-done.5, bf16[27,512,128]{2,1,0:T(8,128)(2,1)S(1)} %bitcast.4), custom_call_target="tpu_custom_call" | custom-call | flops 1073741824 | bytes 3538944 | tf_op jit(solution)/shard_map/send/pallas_call | solution.py:290
  35.4 0.0 copy-start.2
  35.4 1.3 %copy-done.2 = bf16[16,528,128]{2,1,0:T(8,128)(2,1)} copy-done((bf16[16,528,128]{2,1,0:T(8,128)(2,1)}, bf16[16,528,128]{2,1,0:T(8,128)(2,1)S(1)}, u32[]{:S(2)}) %copy-start.2) | copy-done | bytes 2162712
  36.8 8.9 %all-to-all-done.1.data_ref = bf16[16,416,128]{2,1,0:T(8,128)(2,1)} async-done(((bf16[16,416,128]{2,1,0:T(8,128)(2,1)}), bf16[16,416,128]{2,1,0:T(8,128)(2,1)}, u32[]{:S(2)}, u32[]{:S(2)}) %all-to-all-start.1) | async-done | bytes 1703968 | tf_op jit(solution)/shard_map/all_to_all | solution.py:309
  45.7 3.7 %all-to-all-start = ((bf16[16,528,128]{2,1,0:T(8,128)(2,1)}), bf16[16,528,128]{2,1,0:T(8,128)(2,1)S(1)}, u32[]{:S(2)}, u32[]{:S(2)}) async-start(bf16[16,528,128]{2,1,0:T(8,128)(2,1)} %copy-done.2), calls=%async_computation | async-start | bytes 4325376 | tf_op jit(solution)/shard_map/all_to_all | solution.py:309
  49.4 10.3 %tally_tail.1.tail_ref = bf16[32,96,128]{2,1,0:T(8,128)(2,1)S(1)} custom-call(bf16[16,416,128]{2,1,0:T(8,128)(2,1)} %all-to-all-done.1.data_ref), custom_call_target="tpu_custom_call" | custom-call | flops 805306368 | bytes 4194304 | tf_op jit(solution)/shard_map/tally_tail/pallas_call | solution.py:317
  59.7 20.2 %all-to-all-done.data_ref = bf16[16,528,128]{2,1,0:T(8,128)(2,1)S(1)} async-done(((bf16[16,528,128]{2,1,0:T(8,128)(2,1)}), bf16[16,528,128]{2,1,0:T(8,128)(2,1)S(1)}, u32[]{:S(2)}, u32[]{:S(2)}) %all-to-all-start) | async-done | bytes 2162720 | tf_op jit(solution)/shard_map/all_to_all | solution.py:309
  79.9 4.2 %tally.1 = bf16[32,224,128]{2,1,0:T(8,128)(2,1)S(1)} custom-call(bf16[16,528,128]{2,1,0:T(8,128)(2,1)S(1)} %all-to-all-done.data_ref, bf16[32,96,128]{2,1,0:T(8,128)(2,1)S(1)} %tally_tail.1.tail_ref), custom_call_target="tpu_custom_call" | custom-call | flops 805306368 | bytes 4194304 | tf_op jit(solution)/shard_map/tally/pallas_call | solution.py:337
  84.1 47.1 %all_to_all.15 = bf16[32,224,128]{2,1,0:T(8,128)(2,1)S(1)} all-to-all(bf16[32,224,128]{2,1,0:T(8,128)(2,1)S(1)} %tally.1), channel_id=1, replica_groups=mesh['tab'=8,'rep'=4] {'tab','rep'}, dimensions={0} | all-to-all | bytes 3670016 | tf_op jit(solution)/shard_map/all_to_all | solution.py:309
  131.1 1.6 %finish.1 = f32[26,128,128]{2,1,0:T(8,128)} custom-call(bf16[2,16,224,128]{3,2,1,0:T(8,128)(2,1)S(1)} %bitcast.5), custom_call_target="tpu_custom_call" | custom-call | tf_op jit(solution)/shard_map/finish/pallas_call | solution.py:352
  (2 shorter events, 0.0 us)
Async XLA Ops:
  0.6 2.0 %copy-start = (bf16[512,27,128]{2,0,1:T(8,128)(2,1)S(1)}, bf16[512,27,128]{2,0,1:T(8,128)(2,1)}, u32[]{:S(2)}) copy-start(bf16[512,27,128]{2,0,1:T(8,128)(2,1)} %param.4) | copy-start | bytes 10616836
  2.6 1.0 copy-start.4
  3.6 0.8 copy-start.6
  4.5 16.8 %copy-start.1 = (bf16[512,27,128]{2,0,1:T(8,128)(2,1)S(1)}, bf16[512,27,128]{2,0,1:T(8,128)(2,1)}, u32[]{:S(2)}) copy-start(bf16[512,27,128]{2,0,1:T(8,128)(2,1)} %param.4) | copy-start | bytes 10616836
  13.7 1.2 copy-start.3
  14.8 30.8 %all-to-all-start.1 = ((bf16[16,416,128]{2,1,0:T(8,128)(2,1)}), bf16[16,416,128]{2,1,0:T(8,128)(2,1)}, u32[]{:S(2)}, u32[]{:S(2)}) async-start(bf16[16,416,128]{2,1,0:T(8,128)(2,1)} %copy-done.3), calls=%async_computation.1 | async-start | bytes 3407872 | tf_op jit(solution)/shard_map/all_to_all | solution.py:309
  21.2 1.0 copy-start.5
  22.2 0.8 copy-start.7
  35.4 1.4 %copy-start.2 = (bf16[16,528,128]{2,1,0:T(8,128)(2,1)}, bf16[16,528,128]{2,1,0:T(8,128)(2,1)S(1)}, u32[]{:S(2)}) copy-start(bf16[16,528,128]{2,1,0:T(8,128)(2,1)S(1)} %send.2) | copy-start | bytes 6488068
  45.7 34.2 %all-to-all-start = ((bf16[16,528,128]{2,1,0:T(8,128)(2,1)}), bf16[16,528,128]{2,1,0:T(8,128)(2,1)S(1)}, u32[]{:S(2)}, u32[]{:S(2)}) async-start(bf16[16,528,128]{2,1,0:T(8,128)(2,1)} %copy-done.2), calls=%async_computation | async-start | bytes 4325376 | tf_op jit(solution)/shard_map/all_to_all | solution.py:309

commit v5 on v4

--- a/solution.py
+++ b/solution.py
@@ -15,6 +15,8 @@
 HALVES = 2
 PARTS = 4
 GROUP = LANES // PARTS
+GROUP_UNROLL = 8
+EXACT = 256
 
 
 def iota(shape, dim):
@@ -87,12 +89,22 @@
     return jnp.where(group == PARTS - 1, jnp.concatenate(tails, axis=0), out)
 
 
-def send_kernel(first, count, tail, owners, window, ids_ref, pairs_ref, feat_ref, *rest):
+def send_kernel(first, count, tail, owners, window, ids_hbm, pairs_hbm, feat_hbm, *rest):
     if tail:
-        dense_ref, payload_ref, rank_ref, mine, weights, grads = rest
+        payload_hbm, *rest = rest
     else:
-        payload_ref, rank_ref, mine, weights, grads = rest
-    dense = tail
+        dense_ref, payload_hbm, *rest = rest
+    ids_ref, pairs_ref, feat_ref, payload_ref, rank_ref, mine, weights, grads, in_done, out_done = rest
+    inputs = [
+        pltpu.make_async_copy(source, target, in_done.at[at])
+        for at, (source, target) in enumerate([(ids_hbm, ids_ref), (pairs_hbm, pairs_ref), (feat_hbm, feat_ref)])
+    ]
+    for copy in inputs:
+        copy.start()
+
+    def leave(at):
+        return pltpu.make_async_copy(payload_ref.at[at], payload_hbm.at[at], out_done.at[at])
+
     vectors, samples, depth = feat_ref.shape
     span = 2 * LANES
     body = samples * (PARTS - 1) // PARTS if tail else samples
@@ -102,6 +114,7 @@
         payload_ref[at, body:] = jnp.zeros((payload_ref.shape[1] - body, LANES), jnp.bfloat16)
     for at in range(whole, payload_ref.shape[0]):
         payload_ref[at, :body] = jnp.zeros((body, LANES), jnp.bfloat16)
+        leave(at).start()
 
     def store(at, row):
         payload_ref[at, body : body + extra, :] = row
@@ -110,8 +123,10 @@
             place = body + at % 2 * extra
             payload_ref[count + at // 2, place : place + extra, :] = row
 
+    inputs[0].wait()
     order_fields(first, count, owners, window, ids_ref, store, rank_ref, mine)
-    targets = ([0] if dense else []) + list(range(first + 1, first + 1 + count))
+    targets = ([] if tail else [0]) + list(range(first + 1, first + 1 + count))
+    inputs[1].wait()
     pairs = pairs_ref[...].astype(jnp.float32).T.astype(jnp.bfloat16)
     pair_at = iota((pairs.shape[1], span), 0)
     source = iota((1, span), 1) // SUB
@@ -127,6 +142,7 @@
         low = spread_of(targets[at])
         high = spread_of(targets[at + 1]) if at + 1 < len(targets) else jnp.zeros_like(low)
         weights[:, at // 2] = jnp.concatenate([low, high], axis=1).astype(jnp.bfloat16) * own_lane
+    inputs[2].wait()
 
     def per_group(group, carry):
         begin = pl.multiple_of(group * PACK, PACK)
@@ -139,17 +155,23 @@
             out = jnp.dot(left, right.astype(jnp.bfloat16), preferred_element_type=jnp.float32)
             outs.append(out.reshape(-1, SUB, depth))
         out = jnp.concatenate(outs, axis=1)
-        if dense:
+        if not tail:
             dense_ref[pl.ds(begin, PACK), :] = out[0]
             out = out[1:]
         grads[:, pl.ds(begin, PACK), :] = out[:count].astype(jnp.bfloat16)
         return carry
 
-    lax.fori_loop(0, samples // PACK, per_group, 0, unroll=2)
-    slot_at = iota((samples, samples), 0).astype(jnp.float32)
+    lax.fori_loop(0, samples // PACK, per_group, 0, unroll=GROUP_UNROLL)
+    near = math.gcd(samples, EXACT)
+    slot_at = iota((near, samples), 0).astype(jnp.float32).astype(jnp.bfloat16)
 
     def placed(at):
-        placing = one_hot(slot_at == rank_ref[pl.ds(at, 1), :])
+        rank = rank_ref[pl.ds(at, 1), :]
+        tiles = []
+        for top in range(0, samples, near):
+            here = jnp.broadcast_to((rank - top).astype(jnp.bfloat16), (near, samples))
+            tiles.append(jnp.where(slot_at == here, jnp.bfloat16(1), jnp.bfloat16(0)))
+        placing = jnp.concatenate(tiles, axis=0)
         return jnp.dot(placing, grads[at], preferred_element_type=jnp.float32)
 
     if tail:
@@ -157,14 +179,19 @@
             blocks = [placed(each) for each in range(at, min(at + 2, count))]
             for each, block in enumerate(blocks):
                 payload_ref[at + each, :body, :] = fold(block).astype(jnp.bfloat16)
+                leave(at + each).start()
             payload_ref[count + at // 2, :body, :] = fold_last(blocks).astype(jnp.bfloat16)
+            leave(count + at // 2).start()
     else:
 
         def per_field(at, carry):
             payload_ref[at, :body, :] = placed(at).astype(jnp.bfloat16)
+            leave(at).start()
             return carry
 
         lax.fori_loop(0, count, per_field, 0, unroll=2)
+    for at in range(payload_ref.shape[0]):
+        leave(at).wait()
 
 
 def read_tags(window, blocks, first_row, data_ref, tags, tiles):
@@ -274,7 +301,7 @@
     every = ("tab", "rep")
     groups = [list(range(start, start + inner)) for start in range(0, owners, inner)]
     vmem = pl.BlockSpec(memory_space=pltpu.VMEM)
-    params = pltpu.CompilerParams(vmem_limit_bytes=40 * 2**20)
+    params = pltpu.CompilerParams(vmem_limit_bytes=63 * 2**20)
     ids = sample_ids.T
     by_vector = features.transpose(1, 0, 2)
     tail_samples = samples * (PARTS - 1) // PARTS
@@ -282,21 +309,29 @@
     tag_shape = (owners, -(-inner * window // LANES) * LANES)
 
     def send(first, count, is_tail):
-        targets = count + is_tail
+        targets = count + 1 - is_tail
         rows = tail_samples + 2 * extra if is_tail else samples + extra
         shapes = [jax.ShapeDtypeStruct((inner, rows, depth), jnp.bfloat16)]
-        if is_tail:
+        specs = [pl.BlockSpec(memory_space=pl.ANY)]
+        if not is_tail:
             shapes = [jax.ShapeDtypeStruct((samples, depth), jnp.float32)] + shapes
+            specs = [vmem] + specs
         return pl.pallas_call(
             functools.partial(send_kernel, first, count, is_tail, owners, window),
             out_shape=shapes,
-            in_specs=[vmem] * 3,
-            out_specs=[vmem] * len(shapes),
+            in_specs=[pl.BlockSpec(memory_space=pl.ANY)] * 3,
+            out_specs=specs,
             scratch_shapes=[
+                pltpu.VMEM(ids.shape, ids.dtype),
+                pltpu.VMEM(pair_grad.shape, pair_grad.dtype),
+                pltpu.VMEM(by_vector.shape, by_vector.dtype),
+                pltpu.VMEM((inner, rows, depth), jnp.bfloat16),
                 pltpu.VMEM((count, samples), jnp.float32),
                 pltpu.VMEM((count * owners, samples), jnp.bfloat16),
                 pltpu.VMEM((samples // SUB, -(-targets // 2), PACK, 2 * LANES), jnp.bfloat16),
                 pltpu.VMEM((count, samples, depth), jnp.bfloat16),
+                pltpu.SemaphoreType.DMA((3,)),
+                pltpu.SemaphoreType.DMA((inner,)),
             ],
             cost_estimate=pl.CostEstimate(
                 flops=2 * targets * samples * samples * depth, bytes_accessed=2 * features.size, transcendentals=0
@@ -312,8 +347,8 @@
     cost = pl.CostEstimate(
         flops=2 * owners * inner * window * RQ * depth, bytes_accessed=4 * inner * samples * depth, transcendentals=0
     )
-    dense_grad, sent_tail = send(inner, tail, True)
-    arrived_tail = exchange(sent_tail, groups)
+    arrived_tail = exchange(send(inner, tail, True)[0], groups)
+    dense_grad, sent = send(0, inner, False)
     rows_tail = pl.pallas_call(
         functools.partial(tally_tail_kernel, window, samples),
         out_shape=jax.ShapeDtypeStruct((owners, tail_rows, depth), jnp.bfloat16),
@@ -333,7 +368,7 @@
         compiler_params=small,
         name="tally_tail",
     )(arrived_tail)
-    arrived = exchange(send(0, inner, False)[0], groups)
+    arrived = exchange(sent, groups)
     rows = pl.pallas_call(
         functools.partial(tally_kernel, window, samples),
         out_shape=jax.ShapeDtypeStruct((owners, RQ + tail_rows, depth), jnp.bfloat16),

time: 133 us -> 128 us (0.962)
  local copies, waits for them, and re-layouts: 8.17 us -> 0 us
  waiting for transfers between devices: 29.1 us -> 31.3 us
    unnamed x16 -> x0, local copies, waits for them, and re-layouts: 8.17 us -> none
    all_to_all x2, waiting for transfers between devices: 29.1 us -> 31.3 us  [exchange(): lax.all_to_all(blocks, every, split_axis=0, concat_axis=0, tiled=True, ax...]
where the time goes in v5:
time: 128 us; the launch traced here: 127 us
  blocking collectives  47 us (37%)
  Pallas kernels  38.3 us (30%)
  waiting for transfers between devices  31.3 us (24%)
  starting transfers between devices  10.1 us (8%)
    all_to_all x1, blocking collectives, exchange(): lax.all_to_all(blocks, every, split_axis=0, concat_axis=0, tiled=True, ax...  47 us
    all_to_all x2, waiting for transfers between devices, exchange(): lax.all_to_all(blocks, every, split_axis=0, concat_axis=0, tiled=True, ax...  31.3 us
    pallas_call x2, Pallas kernels, send(): pl.pallas_call(functools.partial(send_kernel, first, count, is_tail, owne...  22.3 us
    pallas_call x1, Pallas kernels, local(): pl.pallas_call(functools.partial(tally_tail_kernel, window, samples), out...  10.3 us
    all_to_all x2, starting transfers between devices, exchange(): lax.all_to_all(blocks, every, split_axis=0, concat_axis=0, tiled=True, ax...  10.1 us
    pallas_call x1, Pallas kernels, local(): pl.pallas_call(functools.partial(tally_kernel, window, samples), out_shap...  4.2 us
  transfers between devices with their start and end apart: 2, of which 2 were waited for; matrix products, arithmetic and copies ran while one was open for 0% of the time, Pallas kernels for 8%

profile of v5, /device:TPU:0, one launch (start us, length us, event | category | flops | bytes accessed | tf_op | source)
XLA Modules:
  0.0 127.4 jit_solution(616219159224223873)
XLA Ops:
  0.6 8.9 %send.3 = bf16[16,416,128]{2,1,0:T(8,128)(2,1)} custom-call(s32[26,512]{1,0:T(8,128)} %bitcast.6, bf16[351,512]{1,0:T(8,128)(2,1)} %pairs_hbm.3, bf16[27,512,128]{2,1,0:T(8,128)(2,1)} %bitcast.4), custom_call_target="tpu_custom_call" | custom-call | flops 671088640 | bytes 3538944 | tf_op jit(solution)/shard_map/send/pallas_call | solution.py:319
  9.6 6.4 %all-to-all-start.1 = ((bf16[16,416,128]{2,1,0:T(8,128)(2,1)}), bf16[16,416,128]{2,1,0:T(8,128)(2,1)}, u32[]{:S(2)}, u32[]{:S(2)}) async-start(bf16[16,416,128]{2,1,0:T(8,128)(2,1)} %send.3), calls=%async_computation.1 | async-start | bytes 3407872 | tf_op jit(solution)/shard_map/all_to_all | solution.py:344
  15.9 13.4 %send.2 = (f32[512,128]{1,0:T(8,128)}, bf16[16,528,128]{2,1,0:T(8,128)(2,1)}) custom-call(s32[26,512]{1,0:T(8,128)} %bitcast.7, bf16[351,512]{1,0:T(8,128)(2,1)} %pairs_hbm.3, bf16[27,512,128]{2,1,0:T(8,128)(2,1)} %bitcast.5), custom_call_target="tpu_custom_call" | custom-call | flops 1140850688 | bytes 3538944 | tf_op jit(solution)/shard_map/send/pallas_call | solution.py:319
  29.3 11.1 %all-to-all-done.1.data_ref = bf16[16,416,128]{2,1,0:T(8,128)(2,1)} async-done(((bf16[16,416,128]{2,1,0:T(8,128)(2,1)}), bf16[16,416,128]{2,1,0:T(8,128)(2,1)}, u32[]{:S(2)}, u32[]{:S(2)}) %all-to-all-start.1) | async-done | bytes 1703968 | tf_op jit(solution)/shard_map/all_to_all | solution.py:344
  40.4 3.7 %all-to-all-start = ((bf16[16,528,128]{2,1,0:T(8,128)(2,1)}), bf16[16,528,128]{2,1,0:T(8,128)(2,1)S(1)}, u32[]{:S(2)}, u32[]{:S(2)}) async-start(bf16[16,528,128]{2,1,0:T(8,128)(2,1)} %get-tuple-element.4), calls=%async_computation | async-start | bytes 4325376 | tf_op jit(solution)/shard_map/all_to_all | solution.py:344
  44.1 10.3 %tally_tail.1.tail_ref = bf16[32,96,128]{2,1,0:T(8,128)(2,1)S(1)} custom-call(bf16[16,416,128]{2,1,0:T(8,128)(2,1)} %all-to-all-done.1.data_ref), custom_call_target="tpu_custom_call" | custom-call | flops 805306368 | bytes 4194304 | tf_op jit(solution)/shard_map/tally_tail/pallas_call | solution.py:352
  54.4 20.2 %all-to-all-done.data_ref = bf16[16,528,128]{2,1,0:T(8,128)(2,1)S(1)} async-done(((bf16[16,528,128]{2,1,0:T(8,128)(2,1)}), bf16[16,528,128]{2,1,0:T(8,128)(2,1)S(1)}, u32[]{:S(2)}, u32[]{:S(2)}) %all-to-all-start) | async-done | bytes 2162720 | tf_op jit(solution)/shard_map/all_to_all | solution.py:344
  74.6 4.2 %tally.1 = bf16[32,224,128]{2,1,0:T(8,128)(2,1)S(1)} custom-call(bf16[16,528,128]{2,1,0:T(8,128)(2,1)S(1)} %all-to-all-done.data_ref, bf16[32,96,128]{2,1,0:T(8,128)(2,1)S(1)} %tally_tail.1.tail_ref), custom_call_target="tpu_custom_call" | custom-call | flops 805306368 | bytes 4194304 | tf_op jit(solution)/shard_map/tally/pallas_call | solution.py:372
  78.8 47.0 %all_to_all.15 = bf16[32,224,128]{2,1,0:T(8,128)(2,1)S(1)} all-to-all(bf16[32,224,128]{2,1,0:T(8,128)(2,1)S(1)} %tally.1), channel_id=1, replica_groups=mesh['tab'=8,'rep'=4] {'tab','rep'}, dimensions={0} | all-to-all | bytes 3670016 | tf_op jit(solution)/shard_map/all_to_all | solution.py:344
  125.9 1.6 %finish.1 = f32[26,128,128]{2,1,0:T(8,128)} custom-call(bf16[2,16,224,128]{3,2,1,0:T(8,128)(2,1)S(1)} %bitcast.3), custom_call_target="tpu_custom_call" | custom-call | tf_op jit(solution)/shard_map/finish/pallas_call | solution.py:387
Async XLA Ops:
  9.6 30.9 %all-to-all-start.1 = ((bf16[16,416,128]{2,1,0:T(8,128)(2,1)}), bf16[16,416,128]{2,1,0:T(8,128)(2,1)}, u32[]{:S(2)}, u32[]{:S(2)}) async-start(bf16[16,416,128]{2,1,0:T(8,128)(2,1)} %send.3), calls=%async_computation.1 | async-start | bytes 3407872 | tf_op jit(solution)/shard_map/all_to_all | solution.py:344
  40.4 34.2 %all-to-all-start = ((bf16[16,528,128]{2,1,0:T(8,128)(2,1)}), bf16[16,528,128]{2,1,0:T(8,128)(2,1)S(1)}, u32[]{:S(2)}, u32[]{:S(2)}) async-start(bf16[16,528,128]{2,1,0:T(8,128)(2,1)} %get-tuple-element.4), calls=%async_computation | async-start | bytes 4325376 | tf_op jit(solution)/shard_map/all_to_all | solution.py:344

commit v6 on v5

--- a/solution.py
+++ b/solution.py
@@ -13,7 +13,7 @@
 PACK = 16
 SUB = 8
 HALVES = 2
-PARTS = 4
+PARTS = 8
 GROUP = LANES // PARTS
 GROUP_UNROLL = 8
 EXACT = 256
@@ -63,30 +63,52 @@
         store(at, row.astype(jnp.bfloat16))
 
 
-def fold(block):
-    kept = block.shape[0] * (PARTS - 1) // PARTS
-    moved = [pltpu.roll(block[kept:], (PARTS - 1 - part) * GROUP, 1) for part in range(PARTS - 1)]
-    last_group = iota((kept, LANES), 1) >= LANES - GROUP
-    return jnp.where(last_group, jnp.concatenate(moved, axis=0), block[:kept])
-
-
-def unfold(block):
-    rows = block.shape[0] // (PARTS - 1)
-    group = iota((rows, LANES), 1) // GROUP
-    parts = [pltpu.roll(block[part * rows : (part + 1) * rows], (part + 1) * GROUP, 1) for part in range(PARTS - 1)]
-    return jnp.where(group == 0, parts[0], jnp.where(group == 1, parts[1], parts[2]))
-
-
-def fold_last(blocks):
-    rows = blocks[0].shape[0] // PARTS
-    kept = rows * (PARTS - 1)
-    group = iota((kept, LANES), 1) // GROUP
-    out = jnp.zeros((kept, LANES), blocks[0].dtype)
-    tails = [jnp.zeros((rows, LANES), blocks[0].dtype)] * (PARTS - 1)
-    for part, block in enumerate(blocks):
-        out = jnp.where(group == part, pltpu.roll(block[:kept], (part + 1) * GROUP, 1), out)
-        tails[part] = block[kept:]
-    return jnp.where(group == PARTS - 1, jnp.concatenate(tails, axis=0), out)
+def lane_group(rows):
+    return iota((rows, LANES), 1) // GROUP
+
+
+def shift(block, groups):
+    return pltpu.roll(block, groups * GROUP % LANES, 1) if groups % PARTS else block
+
+
+def pick(block, first, count, other):
+    group = lane_group(block.shape[0])
+    return jnp.where((group >= first) & (group < first + count), block, other)
+
+
+def fold(block, keep):
+    rows = block.shape[0] // PARTS
+    out = []
+    for part in range(keep):
+        kept = block[part * rows : (part + 1) * rows]
+        for at in range(keep, PARTS):
+            kept = pick(shift(block[at * rows : (at + 1) * rows], at - part), at, 1, kept)
+        out.append(kept)
+    return jnp.concatenate(out, axis=0)
+
+
+def unfold(block, keep):
+    rows = block.shape[0] // keep
+    out = []
+    for at in range(keep, PARTS):
+        moved = jnp.zeros((rows, LANES), block.dtype)
+        for part in range(keep):
+            moved = pick(shift(block[part * rows : (part + 1) * rows], part - at), part, 1, moved)
+        out.append(moved)
+    return jnp.concatenate(out, axis=0)
+
+
+def share_out(count, devices):
+    keep = -(-count * PARTS // devices)
+    rest, others = PARTS - keep, devices - count
+    singles = keep - rest
+    if singles < 0 or (count - others) * rest > others * singles:
+        raise ValueError("unsupported sizes")
+    pieces = [(at, 0, at, keep, 0, rest) for at in range(min(others, count))]
+    for at in range(max(count - others, 0) * rest):
+        slot = at % singles
+        pieces.append((at // singles, 1 + slot, others + at // rest, keep + at % rest, rest + slot, 1))
+    return keep, 1 + singles, pieces
 
 
 def send_kernel(first, count, tail, owners, window, ids_hbm, pairs_hbm, feat_hbm, *rest):
@@ -107,21 +129,17 @@
 
     vectors, samples, depth = feat_ref.shape
     span = 2 * LANES
-    body = samples * (PARTS - 1) // PARTS if tail else samples
+    keep, slots, pieces = share_out(count, payload_ref.shape[0]) if tail else (PARTS, 1, [])
+    body = samples * keep // PARTS
     extra = owners // HALVES
-    whole = count + -(-count // 2) if tail else count
     for at in range(count, payload_ref.shape[0]):
         payload_ref[at, body:] = jnp.zeros((payload_ref.shape[1] - body, LANES), jnp.bfloat16)
-    for at in range(whole, payload_ref.shape[0]):
-        payload_ref[at, :body] = jnp.zeros((body, LANES), jnp.bfloat16)
-        leave(at).start()
 
     def store(at, row):
-        payload_ref[at, body : body + extra, :] = row
-        if tail:
-            payload_ref[at, body + extra :, :] = row
-            place = body + at % 2 * extra
-            payload_ref[count + at // 2, place : place + extra, :] = row
+        homes = [(at, slot) for slot in range(slots)]
+        homes += [(count + device, slot) for device, slot, field, *_ in pieces if field == at]
+        for device, slot in homes:
+            payload_ref[device, body + slot * extra : body + (slot + 1) * extra, :] = row
 
     inputs[0].wait()
     order_fields(first, count, owners, window, ids_ref, store, rank_ref, mine)
@@ -175,13 +193,18 @@
         return jnp.dot(placing, grads[at], preferred_element_type=jnp.float32)
 
     if tail:
-        for at in range(0, count, 2):
-            blocks = [placed(each) for each in range(at, min(at + 2, count))]
-            for each, block in enumerate(blocks):
-                payload_ref[at + each, :body, :] = fold(block).astype(jnp.bfloat16)
-                leave(at + each).start()
-            payload_ref[count + at // 2, :body, :] = fold_last(blocks).astype(jnp.bfloat16)
-            leave(count + at // 2).start()
+        for at in range(count):
+            block = placed(at)
+            grads[at] = block.astype(jnp.bfloat16)
+            payload_ref[at, :body, :] = fold(block, keep).astype(jnp.bfloat16)
+            leave(at).start()
+        for at in range(payload_ref.shape[0] - count):
+            block = jnp.zeros((samples, LANES), jnp.float32)
+            for device, _, field, source, target, groups in pieces:
+                if device == at:
+                    block = pick(shift(grads[field].astype(jnp.float32), target - source), target, groups, block)
+            payload_ref[count + at, :body, :] = fold(block, keep).astype(jnp.bfloat16)
+            leave(count + at).start()
     else:
 
         def per_field(at, carry):
@@ -245,47 +268,46 @@
     lax.fori_loop(0, out_ref.shape[0], per_owner, 0, unroll=4)
 
 
-def tally_tail_kernel(window, samples, data_ref, out_ref, unfolded, tags, tags_b, tiles, tiles_b, tile_at, tile_at_b, done):
+def tally_tail_kernel(window, samples, keep, slots, data_ref, out_ref, unfolded, tags, tiles, *rest):
     blocks = data_ref.shape[0]
-    body = samples * (PARTS - 1) // PARTS
-    read_tags(window, blocks, body, data_ref, tags, tiles)
-    read_tags(window, blocks, body + tiles.shape[0], data_ref, tags_b, tiles_b)
-    copy = pltpu.make_async_copy(tiles, tile_at, done.at[0])
-    copy_b = pltpu.make_async_copy(tiles_b, tile_at_b, done.at[1])
-    copy.start()
-    copy_b.start()
+    half = tiles.shape[1]
+    body = samples * keep // PARTS
+    tile_at, done = rest[:slots], rest[slots]
+    copies = []
+    for slot in range(slots):
+        read_tags(window, blocks, body + slot * half, data_ref, tags.at[slot], tiles.at[slot])
+        copies.append(pltpu.make_async_copy(tiles.at[slot], tile_at[slot], done.at[slot]))
+        copies[-1].start()
     for block in range(blocks):
         unfolded[block, :body, :] = data_ref[block, :body, :]
-        unfolded[block, body:, :] = unfold(data_ref[block, :body, :].astype(jnp.float32)).astype(jnp.bfloat16)
-    copy.wait()
-    copy_b.wait()
-    second = iota((RQ, LANES), 1) // GROUP == 1
+        unfolded[block, body:, :] = unfold(data_ref[block, :body, :].astype(jnp.float32), keep).astype(jnp.bfloat16)
+    for copy in copies:
+        copy.wait()
 
     def per_owner(owner, carry):
-        rows = rows_of(window, owner, unfolded, tags, tile_at)
-        rows_b = rows_of(window, owner, unfolded, tags_b, tile_at_b)
-        out_ref[owner] = fold(jnp.where(second, rows_b, rows)).astype(jnp.bfloat16)
+        rows = rows_of(window, owner, unfolded, tags.at[0], tile_at[0])
+        for slot in range(1, slots):
+            other = rows_of(window, owner, unfolded, tags.at[slot], tile_at[slot])
+            rows = pick(other, PARTS - keep + slot - 1, 1, rows)
+        out_ref[owner] = fold(rows, keep).astype(jnp.bfloat16)
         return carry
 
     lax.fori_loop(0, out_ref.shape[0], per_owner, 0, unroll=2)
 
 
-def finish_kernel(count, data_ref, table_ref):
+def finish_kernel(count, keep, pieces, data_ref, table_ref):
     inner = data_ref.shape[1]
-    kept = RQ * (PARTS - 1) // PARTS
-    rest = RQ - kept
     tails = []
     for at in range(inner):
         total = jnp.sum(data_ref[:, at].astype(jnp.float32), axis=0)
         table_ref[at] = total[:RQ]
-        tails.append(total[RQ:])
-    own = iota((RQ, LANES), 1) < LANES - GROUP
+        tails.append(jnp.concatenate([total[RQ:], unfold(total[RQ:], keep)], axis=0))
     for at in range(count):
-        part, block, other = at % 2, tails[at], tails[count + at // 2]
-        main = jnp.concatenate([block, unfold(block)], axis=0)
-        last = pltpu.roll(other, (PARTS - 1 - part) * GROUP, 1)
-        last = jnp.concatenate([last, other[part * rest : (part + 1) * rest]], axis=0)
-        table_ref[inner + at] = jnp.where(own, main, last)
+        rows = tails[at]
+        for device, _, field, source, target, groups in pieces:
+            if field == at:
+                rows = pick(shift(tails[count + device], source - target), source, groups, rows)
+        table_ref[inner + at] = rows
 
 
 def local(outer, inner, sample_ids, features, pair_grad):
@@ -296,21 +318,21 @@
     window = min(-(-(PACK - 1 + capacity) // PACK) * PACK, samples)
     extra = owners // HALVES
     tail = fields - inner
-    if depth != LANES or not 0 < tail + -(-tail // 2) <= inner:
+    if depth != LANES or not 0 < tail <= inner:
         raise ValueError("unsupported sizes")
+    keep, slots, pieces = share_out(tail, inner)
     every = ("tab", "rep")
     groups = [list(range(start, start + inner)) for start in range(0, owners, inner)]
     vmem = pl.BlockSpec(memory_space=pltpu.VMEM)
     params = pltpu.CompilerParams(vmem_limit_bytes=63 * 2**20)
     ids = sample_ids.T
     by_vector = features.transpose(1, 0, 2)
-    tail_samples = samples * (PARTS - 1) // PARTS
-    tail_rows = RQ * (PARTS - 1) // PARTS
+    tail_rows = RQ * keep // PARTS
     tag_shape = (owners, -(-inner * window // LANES) * LANES)
 
     def send(first, count, is_tail):
         targets = count + 1 - is_tail
-        rows = tail_samples + 2 * extra if is_tail else samples + extra
+        rows = samples * keep // PARTS + slots * extra if is_tail else samples + extra
         shapes = [jax.ShapeDtypeStruct((inner, rows, depth), jnp.bfloat16)]
         specs = [pl.BlockSpec(memory_space=pl.ANY)]
         if not is_tail:
@@ -350,19 +372,16 @@
     arrived_tail = exchange(send(inner, tail, True)[0], groups)
     dense_grad, sent = send(0, inner, False)
     rows_tail = pl.pallas_call(
-        functools.partial(tally_tail_kernel, window, samples),
+        functools.partial(tally_tail_kernel, window, samples, keep, slots),
         out_shape=jax.ShapeDtypeStruct((owners, tail_rows, depth), jnp.bfloat16),
         in_specs=[vmem],
         out_specs=vmem,
         scratch_shapes=[
             pltpu.VMEM((inner, samples, depth), jnp.bfloat16),
-            pltpu.VMEM(tag_shape, jnp.float32),
-            pltpu.VMEM(tag_shape, jnp.float32),
-            pltpu.VMEM((extra, LANES), jnp.int32),
-            pltpu.VMEM((extra, LANES), jnp.int32),
-            pltpu.SMEM((extra, LANES), jnp.int32),
-            pltpu.SMEM((extra, LANES), jnp.int32),
-            pltpu.SemaphoreType.DMA((2,)),
+            pltpu.VMEM((slots,) + tag_shape, jnp.float32),
+            pltpu.VMEM((slots, extra, LANES), jnp.int32),
+            *[pltpu.SMEM((extra, LANES), jnp.int32)] * slots,
+            pltpu.SemaphoreType.DMA((slots,)),
         ],
         cost_estimate=cost,
         compiler_params=small,
@@ -385,7 +404,7 @@
         name="tally",
     )(arrived, rows_tail)
     table_grad = pl.pallas_call(
-        functools.partial(finish_kernel, tail),
+        functools.partial(finish_kernel, tail, keep, pieces),
         out_shape=jax.ShapeDtypeStruct((fields, RQ, depth), jnp.float32),
         in_specs=[vmem],
         out_specs=vmem,

time: 128 us -> 123 us (0.961)
  waiting for transfers between devices: 31.3 us -> 26.3 us
  Pallas kernels: 38.3 us -> 41.5 us
  blocking collectives: 47 us -> 44.4 us
    all_to_all x2, waiting for transfers between devices: 31.3 us -> 26.3 us  [exchange(): lax.all_to_all(blocks, every, split_axis=0, concat_axis=0, tiled=True, ax...]
    pallas_call x2, Pallas kernels: 11.8 us -> 14.5 us  [the longest x1 12.5 us: local(): pl.pallas_call(functools.partial(tally_tail_kernel, window, samples, keep...]
    all_to_all x1, blocking collectives: 47 us -> 44.4 us  [exchange(): lax.all_to_all(blocks, every, split_axis=0, concat_axis=0, tiled=True, ax...]
  transfers between devices with their start and end apart: 2 -> 2, of which waited for: 2 -> 2; matrix products, arithmetic and copies ran while one was open for 0% -> 0% of each run, Pallas kernels for 8% -> 10%
where the time goes in v6:
time: 123 us
  blocking collectives  44.4 us (36%)
  Pallas kernels  41.5 us (34%)
  waiting for transfers between devices  26.3 us (21%)
  starting transfers between devices  10.3 us (8%)
    all_to_all x1, blocking collectives, exchange(): lax.all_to_all(blocks, every, split_axis=0, concat_axis=0, tiled=True, ax...  44.4 us
    all_to_all x2, waiting for transfers between devices, exchange(): lax.all_to_all(blocks, every, split_axis=0, concat_axis=0, tiled=True, ax...  26.3 us
    pallas_call x2, Pallas kernels, send(): pl.pallas_call(functools.partial(send_kernel, first, count, is_tail, owne...  22.8 us
    pallas_call x1, Pallas kernels, local(): pl.pallas_call(functools.partial(tally_tail_kernel, window, samples, keep...  12.5 us
    all_to_all x2, starting transfers between devices, exchange(): lax.all_to_all(blocks, every, split_axis=0, concat_axis=0, tiled=True, ax...  10.3 us
    pallas_call x1, Pallas kernels, local(): pl.pallas_call(functools.partial(tally_kernel, window, samples), out_shap...  4.19 us
  transfers between devices with their start and end apart: 2, of which 2 were waited for; matrix products, arithmetic and copies ran while one was open for 0% of the time, Pallas kernels for 10%

profile of v6, /device:TPU:0, one launch (start us, length us, event | category | flops | bytes accessed | tf_op | source)
XLA Modules:
  0.0 123.1 jit_solution(11066621043410018278)
XLA Ops:
  0.6 9.4 %send.3 = bf16[16,368,128]{2,1,0:T(8,128)(2,1)} custom-call(s32[26,512]{1,0:T(8,128)} %bitcast.6, bf16[351,512]{1,0:T(8,128)(2,1)} %pairs_hbm.3, bf16[27,512,128]{2,1,0:T(8,128)(2,1)} %bitcast.4), custom_call_target="tpu_custom_call" | custom-call | flops 671088640 | bytes 3538944 | tf_op jit(solution)/shard_map/send/pallas_call | solution.py:341
  10.0 6.4 %all-to-all-start.1 = ((bf16[16,368,128]{2,1,0:T(8,128)(2,1)}), bf16[16,368,128]{2,1,0:T(8,128)(2,1)}, u32[]{:S(2)}, u32[]{:S(2)}) async-start(bf16[16,368,128]{2,1,0:T(8,128)(2,1)} %send.3), calls=%async_computation.1 | async-start | bytes 3014656 | tf_op jit(solution)/shard_map/all_to_all | solution.py:366
  16.4 13.4 %send.2 = (f32[512,128]{1,0:T(8,128)}, bf16[16,528,128]{2,1,0:T(8,128)(2,1)}) custom-call(s32[26,512]{1,0:T(8,128)} %bitcast.7, bf16[351,512]{1,0:T(8,128)(2,1)} %pairs_hbm.3, bf16[27,512,128]{2,1,0:T(8,128)(2,1)} %bitcast.5), custom_call_target="tpu_custom_call" | custom-call | flops 1140850688 | bytes 3538944 | tf_op jit(solution)/shard_map/send/pallas_call | solution.py:341
  29.8 8.5 %all-to-all-done.1.data_ref = bf16[16,368,128]{2,1,0:T(8,128)(2,1)} async-done(((bf16[16,368,128]{2,1,0:T(8,128)(2,1)}), bf16[16,368,128]{2,1,0:T(8,128)(2,1)}, u32[]{:S(2)}, u32[]{:S(2)}) %all-to-all-start.1) | async-done | bytes 1507360 | tf_op jit(solution)/shard_map/all_to_all | solution.py:366
  38.3 3.9 %all-to-all-start = ((bf16[16,528,128]{2,1,0:T(8,128)(2,1)}), bf16[16,528,128]{2,1,0:T(8,128)(2,1)S(1)}, u32[]{:S(2)}, u32[]{:S(2)}) async-start(bf16[16,528,128]{2,1,0:T(8,128)(2,1)} %get-tuple-element.4), calls=%async_computation | async-start | bytes 4325376 | tf_op jit(solution)/shard_map/all_to_all | solution.py:366
  42.2 12.5 %tally_tail.1.tail_ref = bf16[32,80,128]{2,1,0:T(8,128)(2,1)S(1)} custom-call(bf16[16,368,128]{2,1,0:T(8,128)(2,1)} %all-to-all-done.1.data_ref), custom_call_target="tpu_custom_call" | custom-call | flops 805306368 | bytes 4194304 | tf_op jit(solution)/shard_map/tally_tail/pallas_call | solution.py:374
  54.7 17.8 %all-to-all-done.data_ref = bf16[16,528,128]{2,1,0:T(8,128)(2,1)S(1)} async-done(((bf16[16,528,128]{2,1,0:T(8,128)(2,1)}), bf16[16,528,128]{2,1,0:T(8,128)(2,1)S(1)}, u32[]{:S(2)}, u32[]{:S(2)}) %all-to-all-start) | async-done | bytes 2162720 | tf_op jit(solution)/shard_map/all_to_all | solution.py:366
  72.5 4.2 %tally.1 = bf16[32,208,128]{2,1,0:T(8,128)(2,1)S(1)} custom-call(bf16[16,528,128]{2,1,0:T(8,128)(2,1)S(1)} %all-to-all-done.data_ref, bf16[32,80,128]{2,1,0:T(8,128)(2,1)S(1)} %tally_tail.1.tail_ref), custom_call_target="tpu_custom_call" | custom-call | flops 805306368 | bytes 4194304 | tf_op jit(solution)/shard_map/tally/pallas_call | solution.py:391
  76.7 44.4 %all_to_all.15 = bf16[32,208,128]{2,1,0:T(8,128)(2,1)S(1)} all-to-all(bf16[32,208,128]{2,1,0:T(8,128)(2,1)S(1)} %tally.1), channel_id=1, replica_groups=mesh['tab'=8,'rep'=4] {'tab','rep'}, dimensions={0} | all-to-all | bytes 3407872 | tf_op jit(solution)/shard_map/all_to_all | solution.py:366
  121.2 2.0 %finish.1 = f32[26,128,128]{2,1,0:T(8,128)} custom-call(bf16[2,16,208,128]{3,2,1,0:T(8,128)(2,1)S(1)} %bitcast.3), custom_call_target="tpu_custom_call" | custom-call | tf_op jit(solution)/shard_map/finish/pallas_call | solution.py:406
Async XLA Ops:
  10.0 28.2 %all-to-all-start.1 = ((bf16[16,368,128]{2,1,0:T(8,128)(2,1)}), bf16[16,368,128]{2,1,0:T(8,128)(2,1)}, u32[]{:S(2)}, u32[]{:S(2)}) async-start(bf16[16,368,128]{2,1,0:T(8,128)(2,1)} %send.3), calls=%async_computation.1 | async-start | bytes 3014656 | tf_op jit(solution)/shard_map/all_to_all | solution.py:366
  38.3 34.2 %all-to-all-start = ((bf16[16,528,128]{2,1,0:T(8,128)(2,1)}), bf16[16,528,128]{2,1,0:T(8,128)(2,1)S(1)}, u32[]{:S(2)}, u32[]{:S(2)}) async-start(bf16[16,528,128]{2,1,0:T(8,128)(2,1)} %get-tuple-element.4), calls=%async_computation | async-start | bytes 4325376 | tf_op jit(solution)/shard_map/all_to_all | solution.py:366

commit v7 on v6

--- a/solution.py
+++ b/solution.py
@@ -15,7 +15,8 @@
 HALVES = 2
 PARTS = 8
 GROUP = LANES // PARTS
-GROUP_UNROLL = 8
+GROUP_UNROLL = 16
+OWNER_UNROLL = 32
 EXACT = 256
 
 
@@ -40,9 +41,13 @@
     below = one_hot(iota((owners, owners), 0) > iota((owners, owners), 1))
     slot_at = iota((LANES, samples), 0).astype(jnp.float32)
     lane = iota((owners // HALVES, LANES), 1)
-    for at in range(count):
+    starts = [
+        jnp.dot(below, held[at * owners : (at + 1) * owners].astype(jnp.bfloat16), preferred_element_type=jnp.float32)
+        for at in range(count)
+    ]
+    placed = []
+    for at, start in enumerate(starts):
         rows = slice(at * owners, (at + 1) * owners)
-        start = jnp.dot(below, held[rows].astype(jnp.bfloat16), preferred_element_type=jnp.float32)
         tile = jnp.minimum(jnp.floor(start * (1.0 / PACK)), float(last_tile))
         hit = mine[rows, :].astype(jnp.float32)
         place = hit * (before[rows] + jnp.concatenate([start] * (samples // LANES), axis=1))
@@ -50,6 +55,9 @@
         rank = jnp.sum(place, axis=0, keepdims=True)
         slot = rank - jnp.sum(base, axis=0, keepdims=True)
         rank_ref[at : at + 1, :] = rank
+        placed.append((tile, slot))
+    for at, (tile, slot) in enumerate(placed):
+        hit = mine[at * owners : (at + 1) * owners, :].astype(jnp.float32)
         tag = (ids_ref[first + at : first + at + 1, :] % RQ + 1).astype(jnp.float32)
         tags = lax.dot_general(
             (hit * tag).astype(jnp.bfloat16),
@@ -142,9 +150,9 @@
             payload_ref[device, body + slot * extra : body + (slot + 1) * extra, :] = row
 
     inputs[0].wait()
+    inputs[1].wait()
     order_fields(first, count, owners, window, ids_ref, store, rank_ref, mine)
     targets = ([] if tail else [0]) + list(range(first + 1, first + 1 + count))
-    inputs[1].wait()
     pairs = pairs_ref[...].astype(jnp.float32).T.astype(jnp.bfloat16)
     pair_at = iota((pairs.shape[1], span), 0)
     source = iota((1, span), 1) // SUB
@@ -265,7 +273,7 @@
         out_ref[owner, :RQ, :] = rows_of(window, owner, data_ref, tags, tile_at).astype(jnp.bfloat16)
         return carry
 
-    lax.fori_loop(0, out_ref.shape[0], per_owner, 0, unroll=4)
+    lax.fori_loop(0, out_ref.shape[0], per_owner, 0, unroll=OWNER_UNROLL)
 
 
 def tally_tail_kernel(window, samples, keep, slots, data_ref, out_ref, unfolded, tags, tiles, *rest):
@@ -295,12 +303,17 @@
     lax.fori_loop(0, out_ref.shape[0], per_owner, 0, unroll=2)
 
 
-def finish_kernel(count, keep, pieces, data_ref, table_ref):
+def finish_kernel(count, keep, pieces, data_ref, table_hbm, table_ref, done):
     inner = data_ref.shape[1]
     tails = []
+
+    def leave(at):
+        return pltpu.make_async_copy(table_ref.at[at], table_hbm.at[at], done.at[at])
+
     for at in range(inner):
         total = jnp.sum(data_ref[:, at].astype(jnp.float32), axis=0)
         table_ref[at] = total[:RQ]
+        leave(at).start()
         tails.append(jnp.concatenate([total[RQ:], unfold(total[RQ:], keep)], axis=0))
     for at in range(count):
         rows = tails[at]
@@ -308,6 +321,9 @@
             if field == at:
                 rows = pick(shift(tails[count + device], source - target), source, groups, rows)
         table_ref[inner + at] = rows
+        leave(inner + at).start()
+    for at in range(table_ref.shape[0]):
+        leave(at).wait()
 
 
 def local(outer, inner, sample_ids, features, pair_grad):
@@ -407,7 +423,8 @@
         functools.partial(finish_kernel, tail, keep, pieces),
         out_shape=jax.ShapeDtypeStruct((fields, RQ, depth), jnp.float32),
         in_specs=[vmem],
-        out_specs=vmem,
+        out_specs=pl.BlockSpec(memory_space=pl.ANY),
+        scratch_shapes=[pltpu.VMEM((fields, RQ, depth), jnp.float32), pltpu.SemaphoreType.DMA((fields,))],
         compiler_params=small,
         name="finish",
     )(exchange(rows, None).reshape(outer, inner, RQ + tail_rows, depth))

time: 123 us -> 121 us (0.984)
  Pallas kernels: 41.5 us -> 37 us
  waiting for transfers between devices: 26.3 us -> 27.7 us
    pallas_call x2, Pallas kernels: 22.8 us -> 20.1 us  [send(): pl.pallas_call(functools.partial(send_kernel, first, count, is_tail, owne...]
    pallas_call x1, Pallas kernels: 4.19 us -> 2.62 us  [local(): pl.pallas_call(functools.partial(tally_kernel, window, samples), out_shap...]
    all_to_all x2, waiting for transfers between devices: 26.3 us -> 27.7 us  [exchange(): lax.all_to_all(blocks, every, split_axis=0, concat_axis=0, tiled=True, ax...]
where the time goes in v7:
time: 121 us; the launch traced here: 120 us
  blocking collectives  44.5 us (37%)
  Pallas kernels  37 us (31%)
  waiting for transfers between devices  27.7 us (23%)
  starting transfers between devices  10.3 us (9%)
    all_to_all x1, blocking collectives, exchange(): lax.all_to_all(blocks, every, split_axis=0, concat_axis=0, tiled=True, ax...  44.5 us
    all_to_all x2, waiting for transfers between devices, exchange(): lax.all_to_all(blocks, every, split_axis=0, concat_axis=0, tiled=True, ax...  27.7 us
    pallas_call x2, Pallas kernels, send(): pl.pallas_call(functools.partial(send_kernel, first, count, is_tail, owne...  20.1 us
    pallas_call x1, Pallas kernels, local(): pl.pallas_call(functools.partial(tally_tail_kernel, window, samples, keep...  12.5 us
    all_to_all x2, starting transfers between devices, exchange(): lax.all_to_all(blocks, every, split_axis=0, concat_axis=0, tiled=True, ax...  10.3 us
    pallas_call x1, Pallas kernels, local(): pl.pallas_call(functools.partial(tally_kernel, window, samples), out_shap...  2.62 us
  transfers between devices with their start and end apart: 2, of which 2 were waited for; matrix products, arithmetic and copies ran while one was open for 0% of the time, Pallas kernels for 10%

profile of v7, /device:TPU:0, one launch (start us, length us, event | category | flops | bytes accessed | tf_op | source)
XLA Modules:
  0.0 120.3 jit_solution(6849159601433865525)
XLA Ops:
  0.6 8.2 %send.3 = bf16[16,368,128]{2,1,0:T(8,128)(2,1)} custom-call(s32[26,512]{1,0:T(8,128)} %bitcast.6, bf16[351,512]{1,0:T(8,128)(2,1)} %pairs_hbm.3, bf16[27,512,128]{2,1,0:T(8,128)(2,1)} %bitcast.4), custom_call_target="tpu_custom_call" | custom-call | flops 671088640 | bytes 3538944 | tf_op jit(solution)/shard_map/send/pallas_call | solution.py:357
  8.9 6.4 %all-to-all-start.1 = ((bf16[16,368,128]{2,1,0:T(8,128)(2,1)}), bf16[16,368,128]{2,1,0:T(8,128)(2,1)}, u32[]{:S(2)}, u32[]{:S(2)}) async-start(bf16[16,368,128]{2,1,0:T(8,128)(2,1)} %send.3), calls=%async_computation.1 | async-start | bytes 3014656 | tf_op jit(solution)/shard_map/all_to_all | solution.py:382
  15.2 11.9 %send.2 = (f32[512,128]{1,0:T(8,128)}, bf16[16,528,128]{2,1,0:T(8,128)(2,1)}) custom-call(s32[26,512]{1,0:T(8,128)} %bitcast.7, bf16[351,512]{1,0:T(8,128)(2,1)} %pairs_hbm.3, bf16[27,512,128]{2,1,0:T(8,128)(2,1)} %bitcast.5), custom_call_target="tpu_custom_call" | custom-call | flops 1140850688 | bytes 3538944 | tf_op jit(solution)/shard_map/send/pallas_call | solution.py:357
  27.2 9.9 %all-to-all-done.1.data_ref = bf16[16,368,128]{2,1,0:T(8,128)(2,1)} async-done(((bf16[16,368,128]{2,1,0:T(8,128)(2,1)}), bf16[16,368,128]{2,1,0:T(8,128)(2,1)}, u32[]{:S(2)}, u32[]{:S(2)}) %all-to-all-start.1) | async-done | bytes 1507360 | tf_op jit(solution)/shard_map/all_to_all | solution.py:382
  37.1 3.9 %all-to-all-start = ((bf16[16,528,128]{2,1,0:T(8,128)(2,1)}), bf16[16,528,128]{2,1,0:T(8,128)(2,1)S(1)}, u32[]{:S(2)}, u32[]{:S(2)}) async-start(bf16[16,528,128]{2,1,0:T(8,128)(2,1)} %get-tuple-element.4), calls=%async_computation | async-start | bytes 4325376 | tf_op jit(solution)/shard_map/all_to_all | solution.py:382
  41.0 12.5 %tally_tail.1.tail_ref = bf16[32,80,128]{2,1,0:T(8,128)(2,1)S(1)} custom-call(bf16[16,368,128]{2,1,0:T(8,128)(2,1)} %all-to-all-done.1.data_ref), custom_call_target="tpu_custom_call" | custom-call | flops 805306368 | bytes 4194304 | tf_op jit(solution)/shard_map/tally_tail/pallas_call | solution.py:390
  53.5 17.8 %all-to-all-done.data_ref = bf16[16,528,128]{2,1,0:T(8,128)(2,1)S(1)} async-done(((bf16[16,528,128]{2,1,0:T(8,128)(2,1)}), bf16[16,528,128]{2,1,0:T(8,128)(2,1)S(1)}, u32[]{:S(2)}, u32[]{:S(2)}) %all-to-all-start) | async-done | bytes 2162720 | tf_op jit(solution)/shard_map/all_to_all | solution.py:382
  71.3 2.6 %tally.1 = bf16[32,208,128]{2,1,0:T(8,128)(2,1)S(1)} custom-call(bf16[16,528,128]{2,1,0:T(8,128)(2,1)S(1)} %all-to-all-done.data_ref, bf16[32,80,128]{2,1,0:T(8,128)(2,1)S(1)} %tally_tail.1.tail_ref), custom_call_target="tpu_custom_call" | custom-call | flops 805306368 | bytes 4194304 | tf_op jit(solution)/shard_map/tally/pallas_call | solution.py:407
  74.0 44.5 %all_to_all.15 = bf16[32,208,128]{2,1,0:T(8,128)(2,1)S(1)} all-to-all(bf16[32,208,128]{2,1,0:T(8,128)(2,1)S(1)} %tally.1), channel_id=1, replica_groups=mesh['tab'=8,'rep'=4] {'tab','rep'}, dimensions={0} | all-to-all | bytes 3407872 | tf_op jit(solution)/shard_map/all_to_all | solution.py:382
  118.4 1.7 %finish.1 = f32[26,128,128]{2,1,0:T(8,128)} custom-call(bf16[2,16,208,128]{3,2,1,0:T(8,128)(2,1)S(1)} %bitcast.3), custom_call_target="tpu_custom_call" | custom-call | tf_op jit(solution)/shard_map/finish/pallas_call | solution.py:422
Async XLA Ops:
  8.9 28.2 %all-to-all-start.1 = ((bf16[16,368,128]{2,1,0:T(8,128)(2,1)}), bf16[16,368,128]{2,1,0:T(8,128)(2,1)}, u32[]{:S(2)}, u32[]{:S(2)}) async-start(bf16[16,368,128]{2,1,0:T(8,128)(2,1)} %send.3), calls=%async_computation.1 | async-start | bytes 3014656 | tf_op jit(solution)/shard_map/all_to_all | solution.py:382
  37.1 34.2 %all-to-all-start = ((bf16[16,528,128]{2,1,0:T(8,128)(2,1)}), bf16[16,528,128]{2,1,0:T(8,128)(2,1)S(1)}, u32[]{:S(2)}, u32[]{:S(2)}) async-start(bf16[16,528,128]{2,1,0:T(8,128)(2,1)} %get-tuple-element.4), calls=%async_computation | async-start | bytes 4325376 | tf_op jit(solution)/shard_map/all_to_all | solution.py:382
